TPU v7x, 32 devices: a whole 2x2x4 slice. The times are simulated.
32 devices in a mesh: gx: 4 (over x, core), gy: 2 (over y), gz: 4 (over z).
Axes of the slice: x: 2, y: 2, z: 4, core: 2. Of those that a mesh axis runs over, the one named last changes fastest.
Arguments:
- velocity: float32 [3, 512, 512], P(None, None, ('gx', 'gy', 'gz')), may hold values from -4 to 4
- inv_density: float32 [512, 512], P(None, ('gx', 'gy', 'gz')), may hold values from 0.25 to 4
- element_place: int32 [512], P(('gx', 'gy', 'gz')), may hold values from 0 to 15, as said below
Outputs:
- advected: float32 [3, 512, 512], P(None, None, ('gx', 'gy', 'gz'))
- pressure: float32 [512, 512], P(None, ('gx', 'gy', 'gz'))
- residual: float32 [512, 512], P(None, ('gx', 'gy', 'gz'))
Inputs may be any that keep to these rules, and one draw needn't show every extreme that they name: `element_place`: within each device's 16 consecutive elements every block position appears exactly once.
All inputs are finite; a program needn't handle non-finite values.
Results may differ from a plain program's by a relative error of at most 0.0003.
Values sent between devices are 32-bit elements; how exact they have to be, the bound alone decides.
A program may use at most 64 MiB of HBM per device.

v0:
```python
import functools

import jax
import jax.numpy as jnp
import numpy as np
from jax import lax
from jax.experimental import pallas as pl
from jax.experimental.pallas import tpu as pltpu
from jax.sharding import PartitionSpec as P

BX = 4
BY = 4
BZ = 1
MESH = pl.DeviceIdType.MESH
AXES = ("gx", "gy", "gz")
ROUNDS = 7

time_step = 0.03
mass_shift = 4.0
inner_nodes = (
    -0.8717401485096066,
    -0.5917001814331423,
    -0.2092992179024789,
    0.2092992179024789,
    0.5917001814331423,
    0.8717401485096066,
)


def legendre_seven(position):
    previous = 1.0
    current_value = position
    for degree_index in range(1, 7):
        following = (
            (2 * degree_index + 1) * position * current_value - degree_index * previous
        ) / (degree_index + 1)
        previous = current_value
        current_value = following
    return current_value


def tables():
    nodes = [-1.0] + list(inner_nodes) + [1.0]
    poly = [legendre_seven(node) for node in nodes]
    weights = np.array([2.0 / (56.0 * value * value) for value in poly])
    derivative = np.zeros((8, 8))
    for i in range(8):
        for j in range(8):
            if i != j:
                derivative[i, j] = poly[i] / (poly[j] * (nodes[i] - nodes[j]))
    derivative[0, 0] = -14.0
    derivative[7, 7] = 14.0
    return weights, derivative.astype(np.float32).astype(np.float64)


def lane_rows(matrix):
    rows = np.zeros((32, 128))
    for t in range(4):
        for u in range(4):
            for h in range(2):
                rows[8 * t + 2 * u, 64 * h : 64 * h + 64] = matrix[2 * t + h, 2 * u + h]
                rows[8 * t + 2 * u + 1, 64 * h : 64 * h + 64] = matrix[2 * t + h, 2 * u + 1 - h]
    return rows


def split_stack(matrix):
    high = np.asarray(matrix, np.float32).astype(jnp.bfloat16)
    low = (np.asarray(matrix, np.float32) - high.astype(np.float32)).astype(jnp.bfloat16)
    return np.concatenate([high, high, low], axis=0)


@functools.cache
def constants():
    weights, d = tables()
    eye2, eye8, eye16 = np.eye(2), np.eye(8), np.eye(16)
    forward = np.concatenate(
        [np.kron(np.kron(eye2, d.T), eye8), np.kron(eye16, d.T)], axis=1
    )
    backward = np.concatenate([np.kron(np.kron(eye2, d), eye8), np.kron(eye16, d)], axis=0)
    square = np.kron(np.kron(eye2, d**2), eye8) + np.kron(eye16, d**2)
    quad = np.einsum("a,b,c->abc", weights, weights, weights).reshape(4, 128)
    rows = np.concatenate(
        [lane_rows(d), lane_rows(d.T), lane_rows(d.T**2), quad, np.zeros((4, 128))], axis=0
    )
    return (
        rows.astype(np.float32),
        split_stack(forward),
        split_stack(backward),
        split_stack(square),
    )


def kernel(
    counts,
    vel_ref,
    den_ref,
    place_ref,
    rows_ref,
    fwd_ref,
    bwd_ref,
    sqr_ref,
    adv_ref,
    pre_ref,
    res_ref,
    send_x,
    send_y,
    send_z,
    recv_xy,
    recv_z,
    sums,
    sums_in,
    send_sem,
    recv_sem,
    sum_send,
    sum_recv,
):
    f32 = jnp.float32
    me = [lax.axis_index(name) for name in AXES]
    has = [(me[i] > 0, me[i] < counts[i] - 1) for i in range(3)]

    def each_other(act):
        for kx in range(counts[0]):
            for ky in range(counts[1]):
                base = (kx * counts[1] + ky) * counts[2]
                first = 0 if base else 1

                def one(kz, _):
                    steps = (kx, ky, kz)
                    device = tuple(lax.rem(me[i] + steps[i], counts[i]) for i in range(3))
                    act(device, base + kz - 1)
                    return 0

                if counts[2] <= 8:
                    for kz in range(first, counts[2]):
                        one(kz, 0)
                else:
                    lax.fori_loop(first, counts[2], one, 0)

    barrier = pltpu.get_barrier_semaphore()

    def greet(device, index):
        pl.semaphore_signal(barrier, inc=1, device_id=device, device_id_type=MESH)

    each_other(greet)
    others = counts[0] * counts[1] * counts[2] - 1

    lane = lax.broadcasted_iota(jnp.int32, (1, 16, 128), 2)
    row = lax.broadcasted_iota(jnp.int32, (1, 16, 128), 1)
    ex, ey = row // BY, row % BY
    node_b, node_c = (lane // 8) % 8, lane % 8

    r16 = lax.broadcasted_iota(jnp.int32, (16, 16), 0)
    l16 = lax.broadcasted_iota(jnp.int32, (16, 16), 1)
    by_lane = jnp.zeros((16, 16), jnp.int32)
    by_row = jnp.zeros((16, 16), jnp.int32)
    for e in range(16):
        by_lane = jnp.where(l16 == e, place_ref[e], by_lane)
        by_row = jnp.where(r16 == e, place_ref[e], by_row)
    to_place = (by_lane == r16).astype(f32)
    to_slot = (by_row == l16).astype(f32)

    def order(matrix, block):
        return jnp.dot(
            matrix, block, precision=lax.Precision.HIGHEST, preferred_element_type=f32
        )

    placed = [order(to_place, vel_ref[i]) for i in range(3)]
    velocity = [
        jnp.stack([placed[i][:, 128 * t : 128 * t + 128] for i in range(3)]) for t in range(4)
    ]
    dens = order(to_place, den_ref[...])
    quad = [rows_ref[96 + t : 97 + t, :].reshape(1, 1, 128) for t in range(4)]
    mobile = [quad[t] * dens[:, 128 * t : 128 * t + 128].reshape(1, 16, 128) for t in range(4)]

    def half(flag):
        return jnp.where(flag, 0.5, 1.0).astype(f32)

    total = [BX * counts[0], BY * counts[1], BZ * counts[2]]
    pos_x, pos_y = ex + me[0] * BX, ey + me[1] * BY
    share_y = half(
        ((node_b == 0) & (pos_y > 0)) | ((node_b == 7) & (pos_y < total[1] - 1))
    )
    pos_z = row * 0 + me[2]
    share_z = half(((node_c == 0) & (pos_z > 0)) | ((node_c == 7) & (pos_z < total[2] - 1)))
    share_yz = share_y * share_z
    share = [share_yz] * 4
    share[0] = share_yz * half((lane < 64) & (pos_x > 0))
    share[3] = share_yz * half((lane >= 64) & (pos_x < total[0] - 1))

    def along_x(base, v):
        swapped = [pltpu.roll(v[t], 64, 2) for t in range(4)]
        out = []
        for t in range(4):
            acc = None
            for u in range(4):
                k = base + 8 * t + 2 * u
                term = (
                    rows_ref[k : k + 1, :].reshape(1, 1, 128) * v[u]
                    + rows_ref[k + 1 : k + 2, :].reshape(1, 1, 128) * swapped[u]
                )
                acc = term if acc is None else acc + term
            out.append(acc)
        return out

    def split(x):
        high = x.astype(jnp.bfloat16)
        low = (x - high.astype(f32)).astype(jnp.bfloat16)
        return jnp.concatenate([high, low, high], axis=1)

    def along_lanes(v, w_ref):
        c = v[0].shape[0]
        x = jnp.concatenate([v[t].reshape(c * 16, -1) for t in range(4)], axis=0)
        y = jnp.dot(split(x), w_ref[...], preferred_element_type=f32)
        return [y[t * c * 16 : (t + 1) * c * 16].reshape(c, 16, -1) for t in range(4)]

    directions = [
        (dx, dy, dz)
        for dx in (-1, 0, 1)
        for dy in (-1, 0, 1)
        for dz in (-1, 0, 1)
        if (dx, dy, dz) != (0, 0, 0)
    ]
    columns = [(dx, dy) for dx in (-1, 1, 0) for dy in (0, -1, 1)]
    cases = []
    if counts[2] > 2:
        cases.append(((-1, 0, 1), jnp.logical_and(has[2][0], has[2][1])))
    if counts[2] > 1:
        cases.append(((-1, 0), jnp.logical_not(has[2][1])))
        cases.append(((0, 1), jnp.logical_not(has[2][0])))
    else:
        cases.append(((0,), me[2] == 0))

    def code(d):
        return (d[0] + 1) * 9 + (d[1] + 1) * 3 + d[2] + 1

    def group(d):
        return (d[0] + 1) * 3 + d[1] + 1 if d[0] or d[1] else 9 + side_of(d[2])

    def exists(d):
        flag = None
        for i in range(3):
            if d[i]:
                here = has[i][1 if d[i] > 0 else 0]
                flag = here if flag is None else jnp.logical_and(flag, here)
        return flag

    def side_of(step):
        return 1 if step > 0 else 0

    def source(r, d, c):
        if d[0]:
            return send_x.at[r, side_of(d[0])]
        if d[1]:
            return send_y.at[r, side_of(d[1])]
        return send_z.at[r, side_of(d[2]), pl.ds(0, c)]

    def target(r, d, c):
        if d[0] or d[1]:
            return recv_xy.at[r, code(d)]
        return recv_z.at[r, side_of(d[2]), pl.ds(0, c)]

    def copy(r, d, c, incoming):
        back = d if incoming else tuple(-i for i in d)
        return pltpu.make_async_remote_copy(
            src_ref=source(r, d, c),
            dst_ref=target(r, back, c),
            send_sem=send_sem.at[group(d)],
            recv_sem=recv_sem.at[r, group(back)],
            device_id=tuple(me[i] + d[i] for i in range(3)),
            device_id_type=MESH,
        )

    def each_column(act):
        for steps, flag in cases:

            @pl.when(flag)
            def _():
                for dx, dy in columns:
                    if dx or dy:

                        @pl.when(exists((dx, dy, 0)))
                        def _():
                            act(dx, dy, steps)

                    else:
                        act(dx, dy, [dz for dz in steps if dz])

    def start(r, c):
        def act(dx, dy, steps):
            for dz in steps:
                copy(r, (dx, dy, dz), c, False).start()

        each_column(act)

    def whole(ref, d, rounds_sem):
        return pltpu.make_async_remote_copy(
            src_ref=ref,
            dst_ref=ref,
            send_sem=send_sem.at[group(d)],
            recv_sem=rounds_sem.at[group(d)],
            device_id=tuple(me[i] + d[i] for i in range(3)),
            device_id_type=MESH,
        )

    def finish(r, c):
        def act(dx, dy, steps):
            if dx or dy:
                d = (dx, dy, 0)
                ref = recv_xy.at[r, pl.ds(code((dx, dy, steps[0])), len(steps))]
                whole(ref, d, recv_sem.at[r]).wait_recv()
            else:
                for dz in steps:
                    copy(r, (0, 0, dz), c, True).wait_recv()

        each_column(act)

    def sent():
        def act(dx, dy, steps):
            if dx or dy:
                d = (dx, dy, 0)
                ref = recv_xy.at[:, pl.ds(code((dx, dy, steps[0])), len(steps))]
                whole(ref, d, recv_sem.at[0]).wait_send()
            else:
                for dz in steps:
                    whole(recv_z.at[pl.ds(0, 2)], (0, 0, dz), recv_sem.at[0]).wait_send()

        each_column(act)

    for d in directions:

        @pl.when(jnp.logical_not(exists(d)))
        def _():
            for r in range(ROUNDS):
                if d[0] or d[1]:
                    recv_xy[r, code(d)] = jnp.zeros((8, 128), f32)
                else:
                    recv_z[r, side_of(d[2])] = jnp.zeros((4, 8, 128), f32)

    sub8 = lax.broadcasted_iota(jnp.int32, (8, 128), 0)
    lane8 = lax.broadcasted_iota(jnp.int32, (8, 128), 1)
    quarter = sub8 // 4 + 2 * (lane8 // 64)
    b8, c8, y8 = (lane8 // 8) % 8, lane8 % 8, sub8 % 4

    def turn(x, shift, axis):
        size = x.shape[axis]
        shift = shift % size
        return pltpu.roll(x, shift, axis) if shift else x

    def requarter(x, k, base):
        if (k ^ base) & 1:
            x = turn(x, 4, 0)
        if (k ^ base) & 2:
            x = turn(x, 64, 1)
        return x

    def z_joined(r, dx, dy):
        mid = recv_xy[r, code((dx, dy, 0))]
        low = turn(recv_xy[r, code((dx, dy, -1))], -7, 1)
        high = turn(recv_xy[r, code((dx, dy, 1))], 7, 1)
        return mid + jnp.where(c8 == 0, low, jnp.where(c8 == 7, high, 0.0))

    def assemble(v, r, hook=None):
        v = list(v)
        c = v[0].shape[0]
        lower, upper = turn(v[0], 64, 2), turn(v[3], 64, 2)
        v[0] = v[0] + jnp.where((lane < 64) & (row >= 4), turn(upper, 4, 1), 0.0)
        v[3] = v[3] + jnp.where((lane >= 64) & (row < 12), turn(lower, -4, 1), 0.0)
        lower = v[0]
        upper = turn(v[0], 72, 2)
        for t in range(1, 4):
            lower = jnp.where(node_b == t, turn(v[t], 8 * t, 2), lower)
            upper = jnp.where(node_b == t, turn(v[t], 72 + 8 * t, 2), upper)
        d_low = jnp.where(ey > 0, turn(upper, 1, 1), 0.0)
        d_high = jnp.where(ey < 3, turn(lower, -1, 1), 0.0)

        def add_y(d_low, d_high):
            for t in range(4):
                low, high = turn(d_low, -8 * t, 2), turn(d_high, 56 - 8 * t, 2)
                v[t] = v[t] + jnp.where(node_b == 0, low, jnp.where(node_b == 7, high, 0.0))

        add_y(d_low, d_high)
        lower, upper = lower + d_low, upper + d_high
        for side in range(2):
            base = 3 * side
            acc = None
            for k in range(c):
                part = requarter(v[3 * side][k, 8 * side : 8 * side + 8], k, base)
                acc = part if acc is None else jnp.where(quarter == k, part, acc)
            send_x[r, side] = acc
        for side, face in ((0, lower), (1, upper)):
            acc = None
            for k in range(c):
                part = jnp.where(b8 < 4, face[k, 0:8], turn(face[k, 8:16], 32, 1))
                part = turn(part, k + 5 * side, 0)
                acc = part if acc is None else jnp.where(y8 == k, part, acc)
            send_y[r, side] = acc
        lower = v[0]
        upper = turn(v[0], -7, 2)
        for t in range(1, 4):
            lower = jnp.where(node_c == t, turn(v[t], t, 2), lower)
            upper = jnp.where(node_c == t, turn(v[t], t - 7, 2), upper)
        for side, face in ((0, lower), (1, upper)):
            for k in range(c):
                send_z[r, side, k] = jnp.where(c8 < 4, face[k, 0:8], turn(face[k, 8:16], 4, 1))
        start(r, c)
        if hook is not None:
            hook()
        finish(r, c)
        for side in range(2):
            dx = 2 * side - 1
            low = turn(turn(z_joined(r, dx, -1), -56, 1), -3, 0)
            high = turn(turn(z_joined(r, dx, 1), 56, 1), 3, 0)
            face = z_joined(r, dx, 0) + jnp.where(
                (y8 == 0) & (b8 == 0), low, jnp.where((y8 == 3) & (b8 == 7), high, 0.0)
            )
            base = 3 * side
            parts = [
                jnp.where(quarter == base, requarter(face, k, base), 0.0) for k in range(c)
            ]
            part = jnp.stack(parts)
            zero = jnp.zeros_like(part)
            pair = [part, zero] if side == 0 else [zero, part]
            v[3 * side] = v[3 * side] + jnp.concatenate(pair, axis=1)
        got = []
        for side in range(2):
            face = z_joined(r, 0, 2 * side - 1)
            parts = []
            for k in range(c):
                part = jnp.where(y8 == 3 * side, turn(face, 3 * side - k, 0), 0.0)
                parts.append(jnp.concatenate([part, turn(part, -32, 1)], axis=0))
            got.append(jnp.stack(parts))
        add_y(got[0], got[1])
        got = []
        for side in range(2):
            face = recv_z[r, side, :c]
            got.append(jnp.concatenate([face, turn(face, -4, 2)], axis=1))
        for t in range(4):
            low, high = turn(got[0], -t, 2), turn(got[1], 7 - t, 2)
            v[t] = v[t] + jnp.where(node_c == 0, low, jnp.where(node_c == 7, high, 0.0))
        return v

    def advect(v):
        dx = along_x(0, v)
        dyz = along_lanes(v, fwd_ref)
        return [
            velocity[t][0:1] * dx[t]
            + velocity[t][1:2] * dyz[t][:, :, :128]
            + velocity[t][2:3] * dyz[t][:, :, 128:]
            for t in range(4)
        ]

    first = advect(velocity)
    diag = []

    def diagonal():
        square_x = along_x(64, mobile)
        square_yz = along_lanes(mobile, sqr_ref)
        diag.extend(mass_shift * quad[t] + square_x[t] + square_yz[t] for t in range(4))

    pl.semaphore_wait(barrier, others)
    first = assemble(first, 0, diagonal)
    k1 = [first[t] * share[t] for t in range(4)]
    total_rate = k1
    v = [velocity[t] - (0.5 * time_step) * k1[t] for t in range(4)]
    for r, step, weight in ((1, 0.5, 2.0), (2, 1.0, 2.0), (3, 0.0, 1.0)):
        g = advect(v)
        if r == 1:
            g = assemble([jnp.concatenate([g[t], diag[t]], axis=0) for t in range(4)], r)
            inverse_jacobi = [1.0 / g[t][3:4] for t in range(4)]
            g = [g[t][0:3] for t in range(4)]
        else:
            g = assemble(g, r)
        g = [g[t] * share[t] for t in range(4)]
        total_rate = [total_rate[t] + weight * g[t] for t in range(4)]
        if step:
            v = [velocity[t] - (step * time_step) * g[t] for t in range(4)]
    advected = [velocity[t] - (time_step / 6.0) * total_rate[t] for t in range(4)]

    dx = along_x(0, [advected[t][0:1] for t in range(4)])
    dyz = along_lanes([advected[t][1:3] for t in range(4)], fwd_ref)
    div = [dx[t] + dyz[t][0:1, :, :128] + dyz[t][1:2, :, 128:] for t in range(4)]
    def put(field):
        return order(to_slot, field)

    def put_advected():
        for i in range(3):
            adv_ref[i] = put(jnp.concatenate([advected[t][i] for t in range(4)], axis=1))

    total_div = assemble(div, 4, put_advected)
    r0 = [total_div[t] * (quad[t] * (-1.0 / time_step)) for t in range(4)]

    def local(v):
        dx = along_x(0, v)
        dyz = along_lanes(v, fwd_ref)
        gx = [mobile[t] * dx[t] for t in range(4)]
        gyz = [
            jnp.concatenate(
                [mobile[t] * dyz[t][:, :, :128], mobile[t] * dyz[t][:, :, 128:]], axis=2
            )
            for t in range(4)
        ]
        bx = along_x(32, gx)
        byz = along_lanes(gyz, bwd_ref)
        return [(mass_shift * quad[t]) * v[t] + bx[t] + byz[t] for t in range(4)]

    def dot_row(a, b, scale=None):
        acc = None
        for t in range(4):
            term = a[t] * b[t]
            if scale is not None:
                term = term * scale[t]
            acc = term if acc is None else acc + term
        return jnp.sum(acc[0], axis=0, keepdims=True)

    z0 = [r0[t] * inverse_jacobi[t] for t in range(4)]
    lz = local(z0)
    rho_row = dot_row(r0, z0, share)
    gamma_row = dot_row(z0, lz)
    s = assemble(lz, 5)
    w = [s[t] * inverse_jacobi[t] for t in range(4)]
    lw = local(w)
    delta_row = dot_row(s, w, share)
    eps_row = dot_row(w, lw)
    partial = jnp.concatenate(
        [rho_row, gamma_row, delta_row, eps_row, jnp.zeros((4, 128), f32)], axis=0
    )
    partial = jnp.sum(partial, axis=1, keepdims=True)
    own = jnp.sum(jnp.where(sub8 == lane8, partial, 0.0), axis=0, keepdims=True)
    sums[...] = own

    def share_sums(device, index):
        pltpu.make_async_remote_copy(
            src_ref=sums,
            dst_ref=sums_in.at[index],
            send_sem=sum_send,
            recv_sem=sum_recv,
            device_id=device,
            device_id_type=MESH,
        ).start()

    each_other(share_sums)
    t_vec = assemble(lw, 6)
    arrived = pltpu.make_async_remote_copy(
        src_ref=sums_in,
        dst_ref=sums_in,
        send_sem=sum_send,
        recv_sem=sum_recv,
        device_id=tuple(lax.rem(me[i] + 1, counts[i]) for i in range(3)),
        device_id_type=MESH,
    )
    arrived.wait_recv()
    joined = own + jnp.sum(sums_in[...], axis=0)
    four = jnp.sum(jnp.where(sub8 == lane8, joined, 0.0), axis=1, keepdims=True)
    rho, gamma, delta, eps = (four[i : i + 1].reshape(1, 1, 1) for i in range(4))
    alpha0 = rho / gamma
    rho1 = rho - 2.0 * alpha0 * gamma + alpha0 * alpha0 * delta
    beta = rho1 / rho
    cross = gamma - alpha0 * delta
    curve = gamma - 2.0 * alpha0 * delta + alpha0 * alpha0 * eps
    curve = curve + 2.0 * beta * cross + beta * beta * gamma
    alpha1 = rho1 / curve
    along = alpha0 + alpha1 * (1.0 + beta)
    side_step = alpha0 * alpha1

    pre_ref[...] = put(
        jnp.concatenate([(along * z0[t] - side_step * w[t])[0] for t in range(4)], axis=1)
    )
    res_ref[...] = put(
        jnp.concatenate(
            [(r0[t] - along * s[t] + side_step * t_vec[t])[0] for t in range(4)], axis=1
        )
    )
    sent()
    arrived.wait_send()


def finish_kernel(adv_ref, pre_ref, res_ref, adv_out, pre_out, res_out):
    adv_out[...] = adv_ref[...]
    pre_out[...] = pre_ref[...]
    res_out[...] = res_ref[...]


def per_device(counts, velocity, inv_density, element_place):
    f32 = jnp.float32
    rows, forward, backward, square = constants()
    elements = element_place.shape[0]
    points = inv_density.shape[0]
    vmem = pl.BlockSpec(memory_space=pltpu.VMEM)
    faces = pltpu.VMEM((ROUNDS, 2, 8, 128), f32)
    faces_z = pltpu.VMEM((ROUNDS, 2, 4, 8, 128), f32)
    dma = pltpu.SemaphoreType.DMA
    others = counts[0] * counts[1] * counts[2] - 1
    shapes = (
        jax.ShapeDtypeStruct((3, elements, points), f32),
        jax.ShapeDtypeStruct((elements, points), f32),
        jax.ShapeDtypeStruct((elements, points), f32),
    )
    computed = pl.pallas_call(
        functools.partial(kernel, counts),
        out_shape=shapes,
        in_specs=[vmem, vmem, pl.BlockSpec(memory_space=pltpu.SMEM), vmem, vmem, vmem, vmem],
        out_specs=(vmem, vmem, vmem),
        scratch_shapes=[
            faces,
            faces,
            faces_z,
            pltpu.VMEM((ROUNDS, 27, 8, 128), f32),
            faces_z,
            pltpu.VMEM((1, 128), f32),
            pltpu.VMEM((others, 1, 128), f32),
            dma((11,)),
            dma((ROUNDS, 11)),
            dma,
            dma,
        ],
        compiler_params=pltpu.CompilerParams(collective_id=0, has_side_effects=True),
    )(
        velocity.transpose(0, 2, 1),
        inv_density.T,
        element_place,
        jnp.asarray(rows),
        jnp.asarray(forward),
        jnp.asarray(backward),
        jnp.asarray(square),
    )
    advected, pressure, residual = pl.pallas_call(
        finish_kernel,
        out_shape=shapes,
        in_specs=[vmem, vmem, vmem],
        out_specs=(vmem, vmem, vmem),
    )(*computed)
    return advected.transpose(0, 2, 1), pressure.T, residual.T


def solution(mesh):
    counts = tuple(mesh.shape[name] for name in AXES)
    placed = (P(None, None, AXES), P(None, AXES), P(AXES))
    return jax.shard_map(
        functools.partial(per_device, counts),
        mesh=mesh,
        in_specs=placed,
        out_specs=(P(None, None, AXES), P(None, AXES), P(None, AXES)),
        check_vma=False,
    )
```

profile of v0, /device:TPU:0, one launch (start us, length us, event | category | flops | bytes accessed | tf_op | source)
XLA Modules:
  0.0 41.3 jit_solution(13617429323750535658)
XLA Ops:
  0.6 39.1 %shard_map.94 = (f32[3,16,512]{2,1,0:T(8,128)}, f32[16,512]{1,0:T(8,128)}, f32[16,512]{1,0:T(8,128)}) custom-call(f32[3,16,512]{2,1,0:T(8,128)} %bitcast.5, f32[16,512]{1,0:T(8,128)} %bitcast.6, s32[16]{0:T(128)} %place_ref.1, f32[104,128]{1,0:T(8,128)} %constant.8.clone.rows_ref, bf16[384,256]{1,0:T(8,128)(2,1)} %constant.9.clone.fwd_ref, ...), custom_call_target="tpu_custom_call" | custom-call | tf_op jit(solution)/shard_map/pallas_call | solution.py:598
  39.8 1.6 %shard_map.95 = (f32[3,16,512]{2,1,0:T(8,128)}, f32[16,512]{1,0:T(8,128)}, f32[16,512]{1,0:T(8,128)}) custom-call(f32[3,16,512]{2,1,0:T(8,128)} %get-tuple-element.9.adv_ref, f32[16,512]{1,0:T(8,128)} %get-tuple-element.10.pre_ref, f32[16,512]{1,0:T(8,128)} %get-tuple-element.11.res_ref), custom_call_target="tpu_custom_call" | custom-call | tf_op jit(solution)/shard_map/pallas_call | solution.py:626
where the time goes:
time: 41.5 us; the launch traced here: 41.3 us
  Pallas kernels  40.7 us (98%)
  between operations  0.64 us (2%)
    pallas_call x1, Pallas kernels, per_device(): pl.pallas_call(functools.partial(kernel, counts), out_shape=shapes, in_sp...  39.1 us
    pallas_call x1, Pallas kernels, per_device(): pl.pallas_call(finish_kernel, out_shape=shapes, in_specs=[vmem, vmem, vme...  1.58 us

commit v1 on v0

--- a/solution.py
+++ b/solution.py
@@ -14,6 +14,7 @@
 MESH = pl.DeviceIdType.MESH
 AXES = ("gx", "gy", "gz")
 ROUNDS = 7
+VMEM_LIMIT = 16 << 20
 
 time_step = 0.03
 mass_shift = 4.0
@@ -136,13 +137,44 @@
                 else:
                     lax.fori_loop(first, counts[2], one, 0)
 
+    directions = [
+        (dx, dy, dz)
+        for dx in (-1, 0, 1)
+        for dy in (-1, 0, 1)
+        for dz in (-1, 0, 1)
+        if (dx, dy, dz) != (0, 0, 0)
+    ]
+
+    def exists(d):
+        flag = None
+        for i in range(3):
+            if d[i]:
+                here = has[i][1 if d[i] > 0 else 0]
+                flag = here if flag is None else jnp.logical_and(flag, here)
+        return flag
+
+    def each_neighbour(act):
+        for d in directions:
+
+            @pl.when(exists(d))
+            def _():
+                act(tuple(me[i] + d[i] for i in range(3)), 0)
+
     barrier = pltpu.get_barrier_semaphore()
 
     def greet(device, index):
         pl.semaphore_signal(barrier, inc=1, device_id=device, device_id_type=MESH)
 
-    each_other(greet)
-    others = counts[0] * counts[1] * counts[2] - 1
+    if max(counts) <= ROUNDS:
+        each_neighbour(greet)
+        greeted = 1
+        for i in range(3):
+            low, high = has[i]
+            greeted = greeted * (1 + low.astype(jnp.int32) + high.astype(jnp.int32))
+        others = greeted - 1
+    else:
+        each_other(greet)
+        others = counts[0] * counts[1] * counts[2] - 1
 
     lane = lax.broadcasted_iota(jnp.int32, (1, 16, 128), 2)
     row = lax.broadcasted_iota(jnp.int32, (1, 16, 128), 1)
@@ -213,13 +245,6 @@
         y = jnp.dot(split(x), w_ref[...], preferred_element_type=f32)
         return [y[t * c * 16 : (t + 1) * c * 16].reshape(c, 16, -1) for t in range(4)]
 
-    directions = [
-        (dx, dy, dz)
-        for dx in (-1, 0, 1)
-        for dy in (-1, 0, 1)
-        for dz in (-1, 0, 1)
-        if (dx, dy, dz) != (0, 0, 0)
-    ]
     columns = [(dx, dy) for dx in (-1, 1, 0) for dy in (0, -1, 1)]
     cases = []
     if counts[2] > 2:
@@ -235,14 +260,6 @@
 
     def group(d):
         return (d[0] + 1) * 3 + d[1] + 1 if d[0] or d[1] else 9 + side_of(d[2])
-
-    def exists(d):
-        flag = None
-        for i in range(3):
-            if d[i]:
-                here = has[i][1 if d[i] > 0 else 0]
-                flag = here if flag is None else jnp.logical_and(flag, here)
-        return flag
 
     def side_of(step):
         return 1 if step > 0 else 0
@@ -613,7 +630,9 @@
             dma,
             dma,
         ],
-        compiler_params=pltpu.CompilerParams(collective_id=0, has_side_effects=True),
+        compiler_params=pltpu.CompilerParams(
+            collective_id=0, has_side_effects=True, vmem_limit_bytes=VMEM_LIMIT
+        ),
     )(
         velocity.transpose(0, 2, 1),
         inv_density.T,
@@ -628,6 +647,7 @@
         out_shape=shapes,
         in_specs=[vmem, vmem, vmem],
         out_specs=(vmem, vmem, vmem),
+        compiler_params=pltpu.CompilerParams(vmem_limit_bytes=VMEM_LIMIT),
     )(*computed)
     return advected.transpose(0, 2, 1), pressure.T, residual.T
 

time: 41.5 us -> 44.3 us (1.067)
  local copies, waits for them, and re-layouts: 0 us -> 5.85 us
  Pallas kernels: 40.7 us -> 37.5 us
    unnamed x0 -> x14, local copies, waits for them, and re-layouts: none -> 5.85 us
    pallas_call x1, Pallas kernels: 39.1 us -> 36.8 us  [per_device(): pl.pallas_call(functools.partial(kernel, counts), out_shape=shapes, in_sp...]
    pallas_call x1, Pallas kernels: 1.58 us -> 0.67 us  [per_device(): pl.pallas_call(finish_kernel, out_shape=shapes, in_specs=[vmem, vmem, vme...]
where the time goes in v1:
time: 44.3 us; the launch traced here: 44 us
  Pallas kernels  37.5 us (85%)
  local copies, waits for them, and re-layouts  5.85 us (13%)
  between operations  0.65 us (1%)
    pallas_call x1, Pallas kernels, per_device(): pl.pallas_call(functools.partial(kernel, counts), out_shape=shapes, in_sp...  36.8 us
    unnamed x14, local copies, waits for them, and re-layouts  5.85 us

profile of v1, /device:TPU:0, one launch (start us, length us, event | category | flops | bytes accessed | tf_op | source)
XLA Modules:
  0.0 44.0 jit_solution(5202539571396652659)
XLA Ops:
  0.6 0.0 copy-start.6
  0.6 0.6 %copy-done.6 = s32[16]{0:T(128)S(1)} copy-done((s32[16]{0:T(128)S(1)}, s32[16]{0:T(128)}, u32[]{:S(2)}) %copy-start.6) | copy-done | bytes 88
  1.3 0.0 copy-start
  1.3 0.9 %copy-done = bf16[768,128]{1,0:T(8,128)(2,1)S(1)} copy-done((bf16[768,128]{1,0:T(8,128)(2,1)S(1)}, bf16[768,128]{1,0:T(8,128)(2,1)}, u32[]{:S(2)}) %copy-start) | copy-done | bytes 196632
  2.2 0.0 copy-start.1
  2.2 0.9 %copy-done.1 = bf16[384,256]{1,0:T(8,128)(2,1)S(1)} copy-done((bf16[384,256]{1,0:T(8,128)(2,1)S(1)}, bf16[384,256]{1,0:T(8,128)(2,1)}, u32[]{:S(2)}) %copy-start.1) | copy-done | bytes 196632
  3.1 0.0 copy-start.2
  3.1 0.9 %copy-done.2 = f32[3,512,16]{1,2,0:T(8,128)S(1)} copy-done((f32[3,512,16]{1,2,0:T(8,128)S(1)}, f32[3,512,16]{1,2,0:T(8,128)}, u32[]{:S(2)}) %copy-start.2) | copy-done | bytes 98328
  4.0 0.0 copy-start.3
  4.0 0.9 %copy-done.3 = bf16[384,128]{1,0:T(8,128)(2,1)S(1)} copy-done((bf16[384,128]{1,0:T(8,128)(2,1)S(1)}, bf16[384,128]{1,0:T(8,128)(2,1)}, u32[]{:S(2)}) %copy-start.3) | copy-done | bytes 98328
  4.9 0.0 copy-start.4
  4.9 0.8 %copy-done.4 = f32[104,128]{1,0:T(8,128)S(1)} copy-done((f32[104,128]{1,0:T(8,128)S(1)}, f32[104,128]{1,0:T(8,128)}, u32[]{:S(2)}) %copy-start.4) | copy-done | bytes 53272
  5.7 0.0 copy-start.5
  5.7 0.8 %copy-done.5 = f32[512,16]{0,1:T(8,128)S(1)} copy-done((f32[512,16]{0,1:T(8,128)S(1)}, f32[512,16]{0,1:T(8,128)}, u32[]{:S(2)}) %copy-start.5) | copy-done | bytes 32792
  6.5 36.8 %shard_map.94 = (f32[3,16,512]{2,1,0:T(8,128)S(1)}, f32[16,512]{1,0:T(8,128)S(1)}, f32[16,512]{1,0:T(8,128)S(1)}) custom-call(f32[3,16,512]{2,1,0:T(8,128)S(1)} %bitcast.5, f32[16,512]{1,0:T(8,128)S(1)} %bitcast.6, s32[16]{0:T(128)S(1)} %copy-done.6, f32[104,128]{1,0:T(8,128)S(1)} %copy-done.4, bf16[384,256]{1,0:T(8,128)(2,1)S(1)} %copy-done.1, ...), custom_call_target="tpu_custom_call" | custom-call | tf_op jit(solution)/shard_map/pallas_call | solution.py:615
  43.3 0.7 %shard_map.95 = (f32[3,16,512]{2,1,0:T(8,128)}, f32[16,512]{1,0:T(8,128)}, f32[16,512]{1,0:T(8,128)}) custom-call(f32[3,16,512]{2,1,0:T(8,128)S(1)} %get-tuple-element.9.adv_ref, f32[16,512]{1,0:T(8,128)S(1)} %get-tuple-element.10.pre_ref, f32[16,512]{1,0:T(8,128)S(1)} %get-tuple-element.11.res_ref), custom_call_target="tpu_custom_call" | custom-call | tf_op jit(solution)/shard_map/pallas_call | solution.py:645
Async XLA Ops:
  0.6 0.7 %copy-start.6 = (s32[16]{0:T(128)S(1)}, s32[16]{0:T(128)}, u32[]{:S(2)}) copy-start(s32[16]{0:T(128)} %place_ref.1) | copy-start | bytes 196
  1.3 0.9 %copy-start = (bf16[768,128]{1,0:T(8,128)(2,1)S(1)}, bf16[768,128]{1,0:T(8,128)(2,1)}, u32[]{:S(2)}) copy-start(bf16[768,128]{1,0:T(8,128)(2,1)} %constant.10.clone.bwd_ref) | copy-start | bytes 589828
  2.2 0.9 %copy-start.1 = (bf16[384,256]{1,0:T(8,128)(2,1)S(1)}, bf16[384,256]{1,0:T(8,128)(2,1)}, u32[]{:S(2)}) copy-start(bf16[384,256]{1,0:T(8,128)(2,1)} %constant.9.clone.fwd_ref) | copy-start | bytes 589828
  3.1 0.9 %copy-start.2 = (f32[3,512,16]{1,2,0:T(8,128)S(1)}, f32[3,512,16]{1,2,0:T(8,128)}, u32[]{:S(2)}) copy-start(f32[3,512,16]{1,2,0:T(8,128)} %param.7) | copy-start | bytes 294916
  4.0 0.9 %copy-start.3 = (bf16[384,128]{1,0:T(8,128)(2,1)S(1)}, bf16[384,128]{1,0:T(8,128)(2,1)}, u32[]{:S(2)}) copy-start(bf16[384,128]{1,0:T(8,128)(2,1)} %constant.11.clone.sqr_ref) | copy-start | bytes 294916
  4.9 0.8 %copy-start.4 = (f32[104,128]{1,0:T(8,128)S(1)}, f32[104,128]{1,0:T(8,128)}, u32[]{:S(2)}) copy-start(f32[104,128]{1,0:T(8,128)} %constant.8.clone.rows_ref) | copy-start | bytes 159748
  5.7 0.8 %copy-start.5 = (f32[512,16]{0,1:T(8,128)S(1)}, f32[512,16]{0,1:T(8,128)}, u32[]{:S(2)}) copy-start(f32[512,16]{0,1:T(8,128)} %param.8) | copy-start | bytes 98308

commit v2 on v1

--- a/solution.py
+++ b/solution.py
@@ -93,13 +93,13 @@
 
 def kernel(
     counts,
-    vel_ref,
-    den_ref,
-    place_ref,
-    rows_ref,
-    fwd_ref,
-    bwd_ref,
-    sqr_ref,
+    vel_hbm,
+    den_hbm,
+    place_hbm,
+    rows_hbm,
+    fwd_hbm,
+    bwd_hbm,
+    sqr_hbm,
     adv_ref,
     pre_ref,
     res_ref,
@@ -114,8 +114,32 @@
     recv_sem,
     sum_send,
     sum_recv,
+    vel_ref,
+    den_ref,
+    place_ref,
+    rows_ref,
+    fwd_ref,
+    bwd_ref,
+    sqr_ref,
+    load_sem,
 ):
     f32 = jnp.float32
+    loads = [
+        pltpu.make_async_copy(source_ref, target_ref, load_sem.at[index])
+        for index, (source_ref, target_ref) in enumerate(
+            (
+                (place_hbm, place_ref),
+                (vel_hbm, vel_ref),
+                (rows_hbm, rows_ref),
+                (fwd_hbm, fwd_ref),
+                (den_hbm, den_ref),
+                (sqr_hbm, sqr_ref),
+                (bwd_hbm, bwd_ref),
+            )
+        )
+    ]
+    for load in loads:
+        load.start()
     me = [lax.axis_index(name) for name in AXES]
     has = [(me[i] > 0, me[i] < counts[i] - 1) for i in range(3)]
 
@@ -181,6 +205,7 @@
     ex, ey = row // BY, row % BY
     node_b, node_c = (lane // 8) % 8, lane % 8
 
+    loads[0].wait()
     r16 = lax.broadcasted_iota(jnp.int32, (16, 16), 0)
     l16 = lax.broadcasted_iota(jnp.int32, (16, 16), 1)
     by_lane = jnp.zeros((16, 16), jnp.int32)
@@ -196,13 +221,13 @@
             matrix, block, precision=lax.Precision.HIGHEST, preferred_element_type=f32
         )
 
+    loads[1].wait()
     placed = [order(to_place, vel_ref[i]) for i in range(3)]
     velocity = [
         jnp.stack([placed[i][:, 128 * t : 128 * t + 128] for i in range(3)]) for t in range(4)
     ]
-    dens = order(to_place, den_ref[...])
+    loads[2].wait()
     quad = [rows_ref[96 + t : 97 + t, :].reshape(1, 1, 128) for t in range(4)]
-    mobile = [quad[t] * dens[:, 128 * t : 128 * t + 128].reshape(1, 16, 128) for t in range(4)]
 
     def half(flag):
         return jnp.where(flag, 0.5, 1.0).astype(f32)
@@ -466,10 +491,18 @@
             for t in range(4)
         ]
 
+    loads[3].wait()
     first = advect(velocity)
     diag = []
+    mobile = []
 
     def diagonal():
+        for load in loads[4:]:
+            load.wait()
+        dens = order(to_place, den_ref[...])
+        mobile.extend(
+            quad[t] * dens[:, 128 * t : 128 * t + 128].reshape(1, 16, 128) for t in range(4)
+        )
         square_x = along_x(64, mobile)
         square_yz = along_lanes(mobile, sqr_ref)
         diag.extend(mass_shift * quad[t] + square_x[t] + square_yz[t] for t in range(4))
@@ -615,7 +648,7 @@
     computed = pl.pallas_call(
         functools.partial(kernel, counts),
         out_shape=shapes,
-        in_specs=[vmem, vmem, pl.BlockSpec(memory_space=pltpu.SMEM), vmem, vmem, vmem, vmem],
+        in_specs=[pl.BlockSpec(memory_space=pltpu.HBM)] * 7,
         out_specs=(vmem, vmem, vmem),
         scratch_shapes=[
             faces,
@@ -629,18 +662,31 @@
             dma((ROUNDS, 11)),
             dma,
             dma,
+            pltpu.VMEM((3, elements, points), f32),
+            pltpu.VMEM((elements, points), f32),
+            pltpu.SMEM((elements,), jnp.int32),
+            pltpu.VMEM(rows.shape, f32),
+            pltpu.VMEM(forward.shape, jnp.bfloat16),
+            pltpu.VMEM(backward.shape, jnp.bfloat16),
+            pltpu.VMEM(square.shape, jnp.bfloat16),
+            dma((7,)),
         ],
         compiler_params=pltpu.CompilerParams(
             collective_id=0, has_side_effects=True, vmem_limit_bytes=VMEM_LIMIT
         ),
     )(
-        velocity.transpose(0, 2, 1),
-        inv_density.T,
-        element_place,
-        jnp.asarray(rows),
-        jnp.asarray(forward),
-        jnp.asarray(backward),
-        jnp.asarray(square),
+        *(
+            pltpu.with_memory_space_constraint(operand, pltpu.HBM)
+            for operand in (
+                velocity.transpose(0, 2, 1),
+                inv_density.T,
+                element_place,
+                jnp.asarray(rows),
+                jnp.asarray(forward),
+                jnp.asarray(backward),
+                jnp.asarray(square),
+            )
+        )
     )
     advected, pressure, residual = pl.pallas_call(
         finish_kernel,

time: 44.3 us -> 38.3 us (0.86)
  local copies, waits for them, and re-layouts: 5.85 us -> 0 us
    unnamed x14 -> x0, local copies, waits for them, and re-layouts: 5.85 us -> none
where the time goes in v2:
time: 38.3 us; the launch traced here: 38.2 us
  Pallas kernels  37.6 us (98%)
  between operations  0.64 us (2%)
    pallas_call x1, Pallas kernels, per_device(): pl.pallas_call(functools.partial(kernel, counts), out_shape=shapes, in_sp...  36.9 us

profile of v2, /device:TPU:0, one launch (start us, length us, event | category | flops | bytes accessed | tf_op | source)
XLA Modules:
  0.0 38.2 jit_solution(7621156474337342636)
XLA Ops:
  0.6 36.9 %shard_map.94 = (f32[3,16,512]{2,1,0:T(8,128)S(1)}, f32[16,512]{1,0:T(8,128)S(1)}, f32[16,512]{1,0:T(8,128)S(1)}) custom-call(f32[3,16,512]{2,1,0:T(8,128)} %bitcast.5, f32[16,512]{1,0:T(8,128)} %bitcast.6, s32[16]{0:T(128)} %place_hbm.1, f32[104,128]{1,0:T(8,128)} %constant.8.clone.rows_hbm, bf16[384,256]{1,0:T(8,128)(2,1)} %constant.9.clone.fwd_hbm, ...), custom_call_target="tpu_custom_call" | custom-call | tf_op jit(solution)/shard_map/pallas_call | solution.py:648
  37.5 0.7 %shard_map.95 = (f32[3,16,512]{2,1,0:T(8,128)}, f32[16,512]{1,0:T(8,128)}, f32[16,512]{1,0:T(8,128)}) custom-call(f32[3,16,512]{2,1,0:T(8,128)S(1)} %get-tuple-element.9.adv_ref, f32[16,512]{1,0:T(8,128)S(1)} %get-tuple-element.10.pre_ref, f32[16,512]{1,0:T(8,128)S(1)} %get-tuple-element.11.res_ref), custom_call_target="tpu_custom_call" | custom-call | tf_op jit(solution)/shard_map/pallas_call | solution.py:691

commit v3 on v2

v3 whole, which is shorter than its diff:
```python
import functools

import jax
import jax.numpy as jnp
import numpy as np
from jax import lax
from jax.experimental import pallas as pl
from jax.experimental.pallas import tpu as pltpu
from jax.sharding import PartitionSpec as P

BX = 4
BY = 4
BZ = 1
MESH = pl.DeviceIdType.MESH
AXES = ("gx", "gy", "gz")
ROUNDS = 7
VMEM_LIMIT = 16 << 20

time_step = 0.03
mass_shift = 4.0
inner_nodes = (
    -0.8717401485096066,
    -0.5917001814331423,
    -0.2092992179024789,
    0.2092992179024789,
    0.5917001814331423,
    0.8717401485096066,
)


def legendre_seven(position):
    previous = 1.0
    current_value = position
    for degree_index in range(1, 7):
        following = (
            (2 * degree_index + 1) * position * current_value - degree_index * previous
        ) / (degree_index + 1)
        previous = current_value
        current_value = following
    return current_value


def tables():
    nodes = [-1.0] + list(inner_nodes) + [1.0]
    poly = [legendre_seven(node) for node in nodes]
    weights = np.array([2.0 / (56.0 * value * value) for value in poly])
    derivative = np.zeros((8, 8))
    for i in range(8):
        for j in range(8):
            if i != j:
                derivative[i, j] = poly[i] / (poly[j] * (nodes[i] - nodes[j]))
    derivative[0, 0] = -14.0
    derivative[7, 7] = 14.0
    return weights, derivative.astype(np.float32).astype(np.float64)


def split_stack(matrix):
    high = np.asarray(matrix, np.float32).astype(jnp.bfloat16)
    low = (np.asarray(matrix, np.float32) - high.astype(np.float32)).astype(jnp.bfloat16)
    return np.concatenate([high, high, low], axis=0)


LANE_NODES = (0, 2, 4, 6, 1, 3, 5, 7)


@functools.cache
def constants():
    weights, d = tables()
    nodes = list(LANE_NODES)
    eye16 = np.eye(16)

    def lanes(matrix):
        return split_stack(np.kron(matrix[np.ix_(nodes, nodes)], eye16))

    plane = np.outer(weights, np.repeat(weights[nodes], 16))
    return plane.astype(np.float32), lanes(d.T), lanes(d), lanes(d**2)


def along_index(matrix, sign, v):
    plus = [v[j] + v[7 - j] for j in range(4)]
    minus = [v[j] - v[7 - j] for j in range(4)]
    out = [None] * 8
    for i in range(4):
        even = odd = None
        for j in range(4):
            p = float(0.5 * (matrix[i, j] + matrix[i, 7 - j])) * plus[j]
            n = float(0.5 * (matrix[i, j] - matrix[i, 7 - j])) * minus[j]
            even = p if even is None else even + p
            odd = n if odd is None else odd + n
        out[i] = even + odd
        out[7 - i] = even - odd if sign > 0 else odd - even
    return out


def kernel(
    counts,
    vel_hbm,
    den_hbm,
    place_hbm,
    plane_hbm,
    fwd_hbm,
    bwd_hbm,
    sqr_hbm,
    adv_ref,
    pre_ref,
    res_ref,
    send_x,
    send_y,
    send_z,
    send_e,
    recv_xy,
    recv_z,
    recv_e,
    work_v,
    work_d,
    work_g,
    work_c,
    sums,
    sums_in,
    send_sem,
    recv_sem,
    sum_send,
    sum_recv,
    vel_ref,
    den_ref,
    place_ref,
    plane_ref,
    fwd_ref,
    bwd_ref,
    sqr_ref,
    load_sem,
):
    f32 = jnp.float32
    loads = [
        pltpu.make_async_copy(source_ref, target_ref, load_sem.at[index])
        for index, (source_ref, target_ref) in enumerate(
            (
                (place_hbm, place_ref),
                (vel_hbm, vel_ref),
                (den_hbm, den_ref),
                (fwd_hbm, fwd_ref),
                (plane_hbm, plane_ref),
                (sqr_hbm, sqr_ref),
                (bwd_hbm, bwd_ref),
            )
        )
    ]
    for load in loads:
        load.start()
    me = [lax.axis_index(name) for name in AXES]
    has = [(me[i] > 0, me[i] < counts[i] - 1) for i in range(3)]
    weights, deriv = tables()
    deriv_t, squared_t = deriv.T, deriv.T**2

    def each_other(act):
        for kx in range(counts[0]):
            for ky in range(counts[1]):
                base = (kx * counts[1] + ky) * counts[2]
                first = 0 if base else 1

                def one(kz, _):
                    steps = (kx, ky, kz)
                    device = tuple(lax.rem(me[i] + steps[i], counts[i]) for i in range(3))
                    act(device, base + kz - 1)
                    return 0

                if counts[2] <= 8:
                    for kz in range(first, counts[2]):
                        one(kz, 0)
                else:
                    lax.fori_loop(first, counts[2], one, 0)

    directions = [
        (dx, dy, dz)
        for dx in (-1, 0, 1)
        for dy in (-1, 0, 1)
        for dz in (-1, 0, 1)
        if (dx, dy, dz) != (0, 0, 0)
    ]

    def exists(d):
        flag = None
        for i in range(3):
            if d[i]:
                here = has[i][1 if d[i] > 0 else 0]
                flag = here if flag is None else jnp.logical_and(flag, here)
        return flag

    peers = {d: (exists(d), tuple(me[i] + d[i] for i in range(3))) for d in directions}
    order_out = sorted(directions, key=lambda d: -sum(abs(i) for i in d))

    barrier = pltpu.get_barrier_semaphore()

    def greet(device, index):
        pl.semaphore_signal(barrier, inc=1, device_id=device, device_id_type=MESH)

    if max(counts) <= ROUNDS:
        for d in directions:

            @pl.when(peers[d][0])
            def _():
                greet(peers[d][1], 0)

        greeted = 1
        for i in range(3):
            low, high = has[i]
            greeted = greeted * (1 + low.astype(jnp.int32) + high.astype(jnp.int32))
        others = greeted - 1
    else:
        each_other(greet)
        others = counts[0] * counts[1] * counts[2] - 1

    sub8 = lax.broadcasted_iota(jnp.int32, (8, 128), 0)
    lane8 = lax.broadcasted_iota(jnp.int32, (8, 128), 1)
    ex, ey = (lane8 // 4) % 4, lane8 % 4
    low_x, high_x = lane8 < 16, lane8 >= 112
    join_low_x, join_high_x = low_x & (ex > 0), high_x & (ex < 3)
    join_low_y, join_high_y = (sub8 == 0) & (ey > 0), (sub8 == 7) & (ey < 3)
    pack_b = lane8 // 16
    pack_low_y, pack_high_y = (pack_b == 0) & (ey > 0), (pack_b == 7) & (ey < 3)
    edge_low_y, edge_high_y = (pack_b == 0) & (ey == 0), (pack_b == 7) & (ey == 3)

    def half(flag):
        return jnp.where(flag, 0.5, 1.0).astype(f32)

    total = [BX * counts[0], BY * counts[1], BZ * counts[2]]
    pos_x, pos_y = ex + me[0] * BX, ey + me[1] * BY
    share_xy = half((low_x & (pos_x > 0)) | (high_x & (pos_x < total[0] - 1)))
    share_xy = share_xy * half(
        ((sub8 == 0) & (pos_y > 0)) | ((sub8 == 7) & (pos_y < total[1] - 1))
    )
    share_xy = share_xy.reshape(1, 8, 128)
    share = [share_xy] * 8
    share[0] = share_xy * half(has[2][0])
    share[7] = share_xy * half(has[2][1])

    def turn(x, shift, axis):
        size = x.shape[axis]
        shift = shift % size
        return pltpu.roll(x, shift, axis) if shift else x

    def rows_of(ref, count):
        return [
            jnp.stack([ref[k, pl.ds(b, 8, stride=8), :] for k in range(count)])
            for b in range(8)
        ]

    def planes_of(ref, count):
        return [
            jnp.stack([ref[k, 8 * c : 8 * c + 8, :] for k in range(count)]) for c in range(8)
        ]

    def put_rows(ref, rows):
        for b in range(8):
            for k in range(rows[b].shape[0]):
                ref[k, pl.ds(b, 8, stride=8), :] = rows[b][k]

    def put_planes(ref, planes):
        for c in range(8):
            for k in range(planes[c].shape[0]):
                ref[k, 8 * c : 8 * c + 8, :] = planes[c][k]

    loads[0].wait()
    r16 = lax.broadcasted_iota(jnp.int32, (16, 16), 0)
    l16 = lax.broadcasted_iota(jnp.int32, (16, 16), 1)
    by_lane = jnp.zeros((16, 16), jnp.int32)
    by_row = jnp.zeros((16, 16), jnp.int32)
    for e in range(16):
        by_lane = jnp.where(l16 == e, place_ref[e], by_lane)
        by_row = jnp.where(r16 == e, place_ref[e], by_row)
    to_place = (by_lane == r16).astype(f32)
    to_slot = (by_row == l16).astype(f32)

    def order(matrix, block):
        return jnp.dot(
            matrix, block, precision=lax.Precision.HIGHEST, preferred_element_type=f32
        )

    lane64 = lax.broadcasted_iota(jnp.int32, (64, 128), 1)

    def take(first, second):
        blocks = [
            order(to_place, field)[:, 128 * t : 128 * t + 128]
            for field in (first, second)
            for t in range(4)
        ]
        turned = jnp.concatenate(blocks, axis=0).T
        top, bottom = turned[:64], turned[64:]
        left = jnp.where(lane64 < 64, top, turn(bottom, 64, 1))
        right = jnp.where(lane64 < 64, turn(top, 64, 1), bottom)
        return left, right

    def give(first, second):
        for k, field in enumerate((first, second)):
            for c in range(8):
                work_d[k, 8 * c : 8 * c + 8, :] = field[c].reshape(8, 128)
        left, right = (
            jnp.concatenate(
                [work_d[k, pl.ds(b, 8, stride=8), :] for b in range(8)], axis=0
            )
            for k in range(2)
        )
        top = jnp.where(lane64 < 64, left, turn(right, 64, 1))
        bottom = jnp.where(lane64 < 64, turn(left, 64, 1), right)
        turned = jnp.concatenate([top, bottom], axis=0).T
        return [
            order(
                to_slot,
                jnp.concatenate(
                    [turned[64 * k + 16 * t : 64 * k + 16 * t + 16] for t in range(4)], axis=1
                ),
            )
            for k in range(2)
        ]

    loads[1].wait()
    loads[2].wait()
    taken = [*take(vel_ref[0], vel_ref[1]), *take(vel_ref[2], den_ref[...])]
    put_rows(
        work_v, [jnp.stack([f[8 * b : 8 * b + 8] for f in taken]) for b in range(8)]
    )
    planes = planes_of(work_v, 4)
    velocity = [planes[c][0:3] for c in range(8)]

    def split(x):
        high = x.astype(jnp.bfloat16)
        low = (x - high.astype(f32)).astype(jnp.bfloat16)
        return jnp.concatenate([high, low, high], axis=1)

    def along_x(v, w_ref):
        c = v[0].shape[0]
        x = jnp.concatenate([v[t].reshape(c * 8, 128) for t in range(8)], axis=0)
        y = jnp.dot(split(x), w_ref[...], preferred_element_type=f32)
        return [y[t * c * 8 : (t + 1) * c * 8].reshape(c, 8, 128) for t in range(8)]

    def along_y(v, matrix, sign):
        c = v[0].shape[0]
        put_planes(work_v, v)
        put_rows(work_d, along_index(matrix, sign, rows_of(work_v, c)))
        return planes_of(work_d, c)

    def code(d):
        return (d[0] + 1) * 9 + (d[1] + 1) * 3 + d[2] + 1

    def side_of(step):
        return 1 if step > 0 else 0

    def column(dx, dy):
        return 3 * (dx + 1) + dy + 1

    def source(r, d, c):
        if not d[0] and not d[1]:
            return send_z.at[r, side_of(d[2]), pl.ds(0, c)]
        if d[2]:
            base = 2 * side_of(d[0]) if d[0] else 4 + 2 * side_of(d[1])
            return send_e.at[r, base + side_of(d[2])]
        return (send_x if d[0] else send_y).at[r, side_of(d[0] if d[0] else d[1])]

    def target(r, d, c):
        if not d[0] and not d[1]:
            return recv_z.at[r, side_of(d[2]), pl.ds(0, c)]
        if d[2]:
            return recv_e.at[r, code(d)]
        return recv_xy.at[r, column(d[0], d[1])]

    def copy(r, d, c, incoming):
        back = d if incoming else tuple(-i for i in d)
        return pltpu.make_async_remote_copy(
            src_ref=source(r, d, c),
            dst_ref=target(r, back, c),
            send_sem=send_sem.at[code(d)],
            recv_sem=recv_sem.at[r, code(back)],
            device_id=peers[d][1],
            device_id_type=MESH,
        )

    def start(r, c):
        for d in order_out:

            @pl.when(peers[d][0])
            def _():
                copy(r, d, c, False).start()

    def finish(r, c):
        for d in order_out[::-1]:

            @pl.when(peers[d][0])
            def _():
                copy(r, d, c, True).wait_recv()

    def sent():
        for d in directions:
            if not d[0] and not d[1]:
                ref = recv_z.at[pl.ds(0, 2)]
            elif d[2]:
                ref = recv_e.at[:, 0]
            else:
                ref = recv_xy.at[:, 0]

            @pl.when(peers[d][0])
            def _():
                pltpu.make_async_remote_copy(
                    src_ref=ref,
                    dst_ref=ref,
                    send_sem=send_sem.at[code(d)],
                    recv_sem=recv_sem.at[0, code(d)],
                    device_id=peers[d][1],
                    device_id_type=MESH,
                ).wait_send()

    def clear():
        for d in directions:

            @pl.when(jnp.logical_not(peers[d][0]))
            def _():
                for r in range(ROUNDS):
                    if not d[0] and not d[1]:
                        recv_z[r, side_of(d[2])] = jnp.zeros((4, 8, 128), f32)
                    elif d[2]:
                        recv_e[r, code(d)] = jnp.zeros((1, 128), f32)
                    else:
                        recv_xy[r, column(d[0], d[1])] = jnp.zeros((8, 128), f32)

    def join_x(v):
        low, high = turn(v, 20, 2), turn(v, -20, 2)
        return v + jnp.where(join_low_x, low, jnp.where(join_high_x, high, 0.0))

    def join_y(v):
        low, high = turn(turn(v, 1, 1), 1, 2), turn(turn(v, -1, 1), -1, 2)
        return v + jnp.where(join_low_y, low, jnp.where(join_high_y, high, 0.0))

    def merge(parts, index, bit=1):
        while len(parts) > 1:
            parts = [
                jnp.where((index & bit) == 0, parts[i], parts[i + 1])
                for i in range(0, len(parts), 2)
            ]
            bit *= 2
        return parts[0]

    def z_joined(r, dx, dy):
        low, high = recv_e[r, code((dx, dy, -1))], recv_e[r, code((dx, dy, 1))]
        return recv_xy[r, column(dx, dy)] + jnp.where(
            sub8 == 0, low, jnp.where(sub8 == 7, high, 0.0)
        )

    def assemble(v, r, hook=None):
        c = v[0].shape[0]
        put_planes(work_g, v)
        rows = [
            [work_g[k, pl.ds(b, 8, stride=8), :] for k in range(c)] for b in range(8)
        ]
        for side in range(2):
            packed = []
            for b in range(8):
                acc = turn(rows[b][0], 16 * b - 124 * side, 1)
                for k in range(1, c):
                    part = turn(rows[b][k], 16 * b + 4 * k - 124 * side, 1)
                    acc = jnp.where(ex == k, part, acc)
                packed.append(acc)
            face = merge(packed, pack_b)
            low, high = turn(face, 17, 1), turn(face, -17, 1)
            face = face + jnp.where(pack_low_y, low, jnp.where(pack_high_y, high, 0.0))
            send_x[r, side] = face
            send_e[r, 2 * side] = face[0:1]
            send_e[r, 2 * side + 1] = face[7:8]
        for side in range(2):
            face = turn(rows[7 * side][0], -3 * side, 1)
            for k in range(1, c):
                face = jnp.where(ey == k, turn(rows[7 * side][k], k - 3 * side, 1), face)
            low, high = turn(face, 20, 1), turn(face, -20, 1)
            face = face + jnp.where(join_low_x, low, jnp.where(join_high_x, high, 0.0))
            send_y[r, side] = face
            send_e[r, 4 + 2 * side] = face[0:1]
            send_e[r, 5 + 2 * side] = face[7:8]
        v = list(v)
        for side in range(2):
            v[7 * side] = join_x(join_y(v[7 * side]))
            send_z[r, side, pl.ds(0, c)] = v[7 * side]
        start(r, c)
        for t in range(1, 7):
            v[t] = join_x(join_y(v[t]))
        if hook is not None:
            hook()
        finish(r, c)
        faces = []
        for dx in (-1, 1):
            low = turn(z_joined(r, dx, -1), 13, 1)
            high = turn(z_joined(r, dx, 1), -13, 1)
            faces.append(
                z_joined(r, dx, 0)
                + jnp.where(edge_low_y, low, jnp.where(edge_high_y, high, 0.0))
            )
        for b in range(8):
            for k in range(c):
                low = turn(faces[0], -16 * b - 4 * k, 1)
                high = turn(faces[1], 124 - 16 * b - 4 * k, 1)
                part = jnp.where(lane8 < 4, low, jnp.where(lane8 >= 124, high, 0.0))
                if b in (0, 7):
                    near = 3 if b else 0
                    face = turn(z_joined(r, 0, 1 if b else -1), near - k, 1)
                    part = part + jnp.where(ey == near, face, 0.0)
                work_c[k, pl.ds(b, 8, stride=8), :] = part
        corrections = planes_of(work_c, c)
        v = [v[t] + corrections[t] for t in range(8)]
        for side in range(2):
            v[7 * side] = v[7 * side] + recv_z[r, side, :c]
        return v

    def advect(v):
        dx = along_x(v, fwd_ref)
        dy = along_y(v, deriv, -1)
        dz = along_index(deriv, -1, v)
        return [
            velocity[t][0:1] * dx[t] + velocity[t][1:2] * dy[t] + velocity[t][2:3] * dz[t]
            for t in range(8)
        ]

    loads[3].wait()
    first = advect(velocity)
    diag, quad, mobile = [], [], []

    def diagonal():
        clear()
        for load in loads[4:]:
            load.wait()
        plane = plane_ref[...].reshape(1, 8, 128)
        quad.extend(plane * float(weights[t]) for t in range(8))
        mobile.extend(quad[t] * planes[t][3:4] for t in range(8))
        square_x = along_x(mobile, sqr_ref)
        square_y = along_y(mobile, squared_t, 1)
        square_z = along_index(squared_t, 1, mobile)
        diag.extend(
            mass_shift * quad[t] + square_x[t] + square_y[t] + square_z[t] for t in range(8)
        )

    pl.semaphore_wait(barrier, others)
    first = assemble(first, 0, diagonal)
    k1 = [first[t] * share[t] for t in range(8)]
    total_rate = k1
    v = [velocity[t] - (0.5 * time_step) * k1[t] for t in range(8)]
    for r, step, weight in ((1, 0.5, 2.0), (2, 1.0, 2.0), (3, 0.0, 1.0)):
        g = advect(v)
        if r == 1:
            g = assemble([jnp.concatenate([g[t], diag[t]], axis=0) for t in range(8)], r)
            inverse_jacobi = [1.0 / g[t][3:4] for t in range(8)]
            g = [g[t][0:3] for t in range(8)]
        else:
            g = assemble(g, r)
        g = [g[t] * share[t] for t in range(8)]
        total_rate = [total_rate[t] + weight * g[t] for t in range(8)]
        if step:
            v = [velocity[t] - (step * time_step) * g[t] for t in range(8)]
    advected = [velocity[t] - (time_step / 6.0) * total_rate[t] for t in range(8)]

    div_x = along_x([advected[t][0:1] for t in range(8)], fwd_ref)
    div_y = along_y([advected[t][1:2] for t in range(8)], deriv, -1)
    div_z = along_index(deriv, -1, [advected[t][2:3] for t in range(8)])
    div = [div_x[t] + div_y[t] + div_z[t] for t in range(8)]

    def put_advected():
        parts = [[advected[t][i] for t in range(8)] for i in range(3)]
        adv_ref[0], adv_ref[1] = give(parts[0], parts[1])
        adv_ref[2], _ = give(parts[2], parts[2])

    total_div = assemble(div, 4, put_advected)
    r0 = [total_div[t] * (quad[t] * (-1.0 / time_step)) for t in range(8)]

    def local(v):
        dx = along_x(v, fwd_ref)
        dy = along_y(v, deriv, -1)
        dz = along_index(deriv, -1, v)
        bx = along_x([mobile[t] * dx[t] for t in range(8)], bwd_ref)
        by = along_y([mobile[t] * dy[t] for t in range(8)], deriv_t, -1)
        bz = along_index(deriv_t, -1, [mobile[t] * dz[t] for t in range(8)])
        return [(mass_shift * quad[t]) * v[t] + bx[t] + by[t] + bz[t] for t in range(8)]

    def dot_row(a, b, scale=None):
        acc = None
        for t in range(8):
            term = a[t] * b[t]
            if scale is not None:
                term = term * scale[t]
            acc = term if acc is None else acc + term
        return jnp.sum(acc[0], axis=0, keepdims=True)

    given = {}

    def give_first():
        given["r0"], given["z0"] = give(r0, z0)

    def give_second():
        given["s"], given["w"] = give(s, w)

    z0 = [r0[t] * inverse_jacobi[t] for t in range(8)]
    lz = local(z0)
    rho_row = dot_row(r0, z0, share)
    gamma_row = dot_row(z0, lz)
    s = assemble(lz, 5, give_first)
    w = [s[t] * inverse_jacobi[t] for t in range(8)]
    lw = local(w)
    delta_row = dot_row(s, w, share)
    eps_row = dot_row(w, lw)
    partial = jnp.concatenate(
        [rho_row, gamma_row, delta_row, eps_row, jnp.zeros((4, 128), f32)], axis=0
    )
    partial = jnp.sum(partial, axis=1, keepdims=True)
    own = jnp.sum(jnp.where(sub8 == lane8, partial, 0.0), axis=0, keepdims=True)
    sums[...] = own

    def share_sums(device, index):
        pltpu.make_async_remote_copy(
            src_ref=sums,
            dst_ref=sums_in.at[index],
            send_sem=sum_send,
            recv_sem=sum_recv,
            device_id=device,
            device_id_type=MESH,
        ).start()

    each_other(share_sums)
    t_vec = assemble(lw, 6, give_second)
    third, _ = give(t_vec, t_vec)
    arrived = pltpu.make_async_remote_copy(
        src_ref=sums_in,
        dst_ref=sums_in,
        send_sem=sum_send,
        recv_sem=sum_recv,
        device_id=tuple(lax.rem(me[i] + 1, counts[i]) for i in range(3)),
        device_id_type=MESH,
    )
    arrived.wait_recv()
    joined = own + jnp.sum(sums_in[...], axis=0)
    four = jnp.sum(jnp.where(sub8 == lane8, joined, 0.0), axis=1, keepdims=True)
    rho, gamma, delta, eps = (four[i : i + 1] for i in range(4))
    alpha0 = rho / gamma
    rho1 = rho - 2.0 * alpha0 * gamma + alpha0 * alpha0 * delta
    beta = rho1 / rho
    cross = gamma - alpha0 * delta
    curve = gamma - 2.0 * alpha0 * delta + alpha0 * alpha0 * eps
    curve = curve + 2.0 * beta * cross + beta * beta * gamma
    alpha1 = rho1 / curve
    along = alpha0 + alpha1 * (1.0 + beta)
    side_step = alpha0 * alpha1

    pre_ref[...] = along * given["z0"] - side_step * given["w"]
    res_ref[...] = given["r0"] - along * given["s"] + side_step * third
    sent()
    arrived.wait_send()


def finish_kernel(adv_ref, pre_ref, res_ref, adv_out, pre_out, res_out):
    adv_out[...] = adv_ref[...]
    pre_out[...] = pre_ref[...]
    res_out[...] = res_ref[...]


def per_device(counts, velocity, inv_density, element_place):
    f32 = jnp.float32
    plane, forward, backward, square = constants()
    elements = element_place.shape[0]
    points = inv_density.shape[0]
    vmem = pl.BlockSpec(memory_space=pltpu.VMEM)
    faces = pltpu.VMEM((ROUNDS, 2, 8, 128), f32)
    faces_z = pltpu.VMEM((ROUNDS, 2, 4, 8, 128), f32)
    work = pltpu.VMEM((4, 64, 128), f32)
    dma = pltpu.SemaphoreType.DMA
    others = counts[0] * counts[1] * counts[2] - 1
    shapes = (
        jax.ShapeDtypeStruct((3, elements, points), f32),
        jax.ShapeDtypeStruct((elements, points), f32),
        jax.ShapeDtypeStruct((elements, points), f32),
    )
    computed = pl.pallas_call(
        functools.partial(kernel, counts),
        out_shape=shapes,
        in_specs=[pl.BlockSpec(memory_space=pltpu.HBM)] * 7,
        out_specs=(vmem, vmem, vmem),
        scratch_shapes=[
            faces,
            faces,
            faces_z,
            pltpu.VMEM((ROUNDS, 8, 1, 128), f32),
            pltpu.VMEM((ROUNDS, 9, 8, 128), f32),
            faces_z,
            pltpu.VMEM((ROUNDS, 27, 1, 128), f32),
            work,
            work,
            work,
            work,
            pltpu.VMEM((1, 128), f32),
            pltpu.VMEM((others, 1, 128), f32),
            dma((27,)),
            dma((ROUNDS, 27)),
            dma,
            dma,
            pltpu.VMEM((3, elements, points), f32),
            pltpu.VMEM((elements, points), f32),
            pltpu.SMEM((elements,), jnp.int32),
            pltpu.VMEM(plane.shape, f32),
            pltpu.VMEM(forward.shape, jnp.bfloat16),
            pltpu.VMEM(backward.shape, jnp.bfloat16),
            pltpu.VMEM(square.shape, jnp.bfloat16),
            dma((7,)),
        ],
        compiler_params=pltpu.CompilerParams(
            collective_id=0, has_side_effects=True, vmem_limit_bytes=VMEM_LIMIT
        ),
    )(
        *(
            pltpu.with_memory_space_constraint(operand, pltpu.HBM)
            for operand in (
                velocity.transpose(0, 2, 1),
                inv_density.T,
                element_place,
                jnp.asarray(plane),
                jnp.asarray(forward),
                jnp.asarray(backward),
                jnp.asarray(square),
            )
        )
    )
    advected, pressure, residual = pl.pallas_call(
        finish_kernel,
        out_shape=shapes,
        in_specs=[vmem, vmem, vmem],
        out_specs=(vmem, vmem, vmem),
        compiler_params=pltpu.CompilerParams(vmem_limit_bytes=VMEM_LIMIT),
    )(*computed)
    return advected.transpose(0, 2, 1), pressure.T, residual.T


def solution(mesh):
    counts = tuple(mesh.shape[name] for name in AXES)
    placed = (P(None, None, AXES), P(None, AXES), P(AXES))
    return jax.shard_map(
        functools.partial(per_device, counts),
        mesh=mesh,
        in_specs=placed,
        out_specs=(P(None, None, AXES), P(None, AXES), P(None, AXES)),
        check_vma=False,
    )
```

time: 38.3 us -> 36.3 us (0.948)
  Pallas kernels: 37.6 us -> 35.5 us
    pallas_call x1, Pallas kernels: 36.9 us -> 34.8 us  [per_device(): pl.pallas_call(functools.partial(kernel, counts), out_shape=shapes, in_sp...]
where the time goes in v3:
time: 36.3 us; the launch traced here: 36.1 us
  Pallas kernels  35.5 us (98%)
  between operations  0.64 us (2%)
    pallas_call x1, Pallas kernels, per_device(): pl.pallas_call(functools.partial(kernel, counts), out_shape=shapes, in_sp...  34.8 us

profile of v3, /device:TPU:0, one launch (start us, length us, event | category | flops | bytes accessed | tf_op | source)
XLA Modules:
  0.0 36.1 jit_solution(14057478793437614189)
XLA Ops:
  0.6 34.8 %shard_map.94 = (f32[3,16,512]{2,1,0:T(8,128)S(1)}, f32[16,512]{1,0:T(8,128)S(1)}, f32[16,512]{1,0:T(8,128)S(1)}) custom-call(f32[3,16,512]{2,1,0:T(8,128)} %bitcast.5, f32[16,512]{1,0:T(8,128)} %bitcast.6, s32[16]{0:T(128)} %place_hbm.1, f32[8,128]{1,0:T(8,128)} %constant.8.clone.plane_hbm, bf16[384,128]{1,0:T(8,128)(2,1)} %constant.9.clone.fwd_hbm, ...), custom_call_target="tpu_custom_call" | custom-call | tf_op jit(solution)/shard_map/pallas_call | solution.py:674
  35.4 0.7 %shard_map.95 = (f32[3,16,512]{2,1,0:T(8,128)}, f32[16,512]{1,0:T(8,128)}, f32[16,512]{1,0:T(8,128)}) custom-call(f32[3,16,512]{2,1,0:T(8,128)S(1)} %get-tuple-element.9.adv_ref, f32[16,512]{1,0:T(8,128)S(1)} %get-tuple-element.10.pre_ref, f32[16,512]{1,0:T(8,128)S(1)} %get-tuple-element.11.res_ref), custom_call_target="tpu_custom_call" | custom-call | tf_op jit(solution)/shard_map/pallas_call | solution.py:723

commit v4 on v3

--- a/solution.py
+++ b/solution.py
@@ -187,7 +187,11 @@
         return flag
 
     peers = {d: (exists(d), tuple(me[i] + d[i] for i in range(3))) for d in directions}
-    order_out = sorted(directions, key=lambda d: -sum(abs(i) for i in d))
+    far = [d for d in directions if d[1] and d[2]]
+    far.sort(key=lambda d: abs(d[0]))
+    near_edges = [d for d in directions if d[0] and d[2] and not d[1]]
+    near = [d for d in directions if d not in far and d not in near_edges]
+    near.sort(key=lambda d: (-abs(d[2]), -abs(d[1]), abs(d[0])))
 
     barrier = pltpu.get_barrier_semaphore()
 
@@ -352,8 +356,8 @@
         if not d[0] and not d[1]:
             return send_z.at[r, side_of(d[2]), pl.ds(0, c)]
         if d[2]:
-            base = 2 * side_of(d[0]) if d[0] else 4 + 2 * side_of(d[1])
-            return send_e.at[r, base + side_of(d[2])]
+            kind = (8 if d[1] else 0) if d[0] else 4
+            return send_e.at[r, kind + 2 * side_of(d[0] or d[1]) + side_of(d[2])]
         return (send_x if d[0] else send_y).at[r, side_of(d[0] if d[0] else d[1])]
 
     def target(r, d, c):
@@ -374,15 +378,15 @@
             device_id_type=MESH,
         )
 
-    def start(r, c):
-        for d in order_out:
+    def start(r, c, group):
+        for d in group:
 
             @pl.when(peers[d][0])
             def _():
                 copy(r, d, c, False).start()
 
-    def finish(r, c):
-        for d in order_out[::-1]:
+    def finish(r, c, group):
+        for d in group[::-1]:
 
             @pl.when(peers[d][0])
             def _():
@@ -438,11 +442,15 @@
             bit *= 2
         return parts[0]
 
-    def z_joined(r, dx, dy):
+    def by_slot(parts, slot):
+        acc = parts[0]
+        for k in range(1, len(parts)):
+            acc = jnp.where(slot == k, parts[k], acc)
+        return acc
+
+    def edge_rows(r, dx, dy):
         low, high = recv_e[r, code((dx, dy, -1))], recv_e[r, code((dx, dy, 1))]
-        return recv_xy[r, column(dx, dy)] + jnp.where(
-            sub8 == 0, low, jnp.where(sub8 == 7, high, 0.0)
-        )
+        return jnp.where(sub8 == 0, low, jnp.where(sub8 == 7, high, 0.0))
 
     def assemble(v, r, hook=None):
         c = v[0].shape[0]
@@ -451,61 +459,76 @@
             [work_g[k, pl.ds(b, 8, stride=8), :] for k in range(c)] for b in range(8)
         ]
         for side in range(2):
-            packed = []
-            for b in range(8):
-                acc = turn(rows[b][0], 16 * b - 124 * side, 1)
-                for k in range(1, c):
-                    part = turn(rows[b][k], 16 * b + 4 * k - 124 * side, 1)
-                    acc = jnp.where(ex == k, part, acc)
-                packed.append(acc)
-            face = merge(packed, pack_b)
+            own = rows[7 * side]
+            face = by_slot([turn(own[k], k - 3 * side, 1) for k in range(c)], ey)
+            low = by_slot([turn(own[k], k - 3 * side + 20, 1) for k in range(c)], ey)
+            high = by_slot([turn(own[k], k - 3 * side - 20, 1) for k in range(c)], ey)
+            face = face + jnp.where(join_low_x, low, jnp.where(join_high_x, high, 0.0))
+            send_y[r, side] = face
+            send_e[r, 4 + 2 * side] = face[0:1]
+            send_e[r, 5 + 2 * side] = face[7:8]
+
+        def pack(side, b):
+            shift = 16 * b - 124 * side
+            return by_slot([turn(rows[b][k], shift + 4 * k, 1) for k in range(c)], ex)
+
+        packed = [[pack(side, b) if b in (0, 7) else None for b in range(8)] for side in range(2)]
+        for side in range(2):
+            corner = jnp.where(pack_b < 4, packed[side][0], packed[side][7])
+            send_e[r, 8 + 2 * side] = corner[0:1]
+            send_e[r, 9 + 2 * side] = corner[7:8]
+        start(r, c, far)
+        v = list(v)
+        for side in range(2):
+            v[7 * side] = join_x(join_y(v[7 * side]))
+            send_z[r, side, pl.ds(0, c)] = v[7 * side]
+        for side in range(2):
+            face = merge(
+                [packed[side][b] if b in (0, 7) else pack(side, b) for b in range(8)], pack_b
+            )
             low, high = turn(face, 17, 1), turn(face, -17, 1)
             face = face + jnp.where(pack_low_y, low, jnp.where(pack_high_y, high, 0.0))
             send_x[r, side] = face
             send_e[r, 2 * side] = face[0:1]
             send_e[r, 2 * side + 1] = face[7:8]
-        for side in range(2):
-            face = turn(rows[7 * side][0], -3 * side, 1)
-            for k in range(1, c):
-                face = jnp.where(ey == k, turn(rows[7 * side][k], k - 3 * side, 1), face)
-            low, high = turn(face, 20, 1), turn(face, -20, 1)
-            face = face + jnp.where(join_low_x, low, jnp.where(join_high_x, high, 0.0))
-            send_y[r, side] = face
-            send_e[r, 4 + 2 * side] = face[0:1]
-            send_e[r, 5 + 2 * side] = face[7:8]
-        v = list(v)
-        for side in range(2):
-            v[7 * side] = join_x(join_y(v[7 * side]))
-            send_z[r, side, pl.ds(0, c)] = v[7 * side]
-        start(r, c)
+        start(r, c, near_edges + near)
         for t in range(1, 7):
             v[t] = join_x(join_y(v[t]))
         if hook is not None:
             hook()
-        finish(r, c)
+        finish(r, c, near)
         faces = []
         for dx in (-1, 1):
-            low = turn(z_joined(r, dx, -1), 13, 1)
-            high = turn(z_joined(r, dx, 1), -13, 1)
+            low = turn(recv_xy[r, column(dx, -1)], 13, 1)
+            high = turn(recv_xy[r, column(dx, 1)], -13, 1)
             faces.append(
-                z_joined(r, dx, 0)
+                recv_xy[r, column(dx, 0)]
                 + jnp.where(edge_low_y, low, jnp.where(edge_high_y, high, 0.0))
             )
-        for b in range(8):
+        for side in range(2):
+            v[7 * side] = v[7 * side] + recv_z[r, side, :c]
+        finish(r, c, far + near_edges)
+        faces = [faces[i] + edge_rows(r, 2 * i - 1, 0) for i in range(2)]
+        sides = [recv_xy[r, column(0, dy)] + edge_rows(r, 0, dy) for dy in (-1, 1)]
+        corners = [[edge_rows(r, dx, dy) for dx in (-1, 1)] for dy in (-1, 1)]
+        for b in (0, 7, 1, 2, 3, 4, 5, 6):
             for k in range(c):
                 low = turn(faces[0], -16 * b - 4 * k, 1)
                 high = turn(faces[1], 124 - 16 * b - 4 * k, 1)
                 part = jnp.where(lane8 < 4, low, jnp.where(lane8 >= 124, high, 0.0))
                 if b in (0, 7):
-                    near = 3 if b else 0
-                    face = turn(z_joined(r, 0, 1 if b else -1), near - k, 1)
-                    part = part + jnp.where(ey == near, face, 0.0)
+                    side = b // 7
+                    slot = 3 * side
+                    part = part + jnp.where(ey == slot, turn(sides[side], slot - k, 1), 0.0)
+                    begin = slot - 4 * k - 115 * (1 - side)
+                    low = turn(corners[side][0], begin, 1)
+                    high = turn(corners[side][1], begin + 124, 1)
+                    part = part + jnp.where(
+                        lane8 == slot, low, jnp.where(lane8 == 124 + slot, high, 0.0)
+                    )
                 work_c[k, pl.ds(b, 8, stride=8), :] = part
         corrections = planes_of(work_c, c)
-        v = [v[t] + corrections[t] for t in range(8)]
-        for side in range(2):
-            v[7 * side] = v[7 * side] + recv_z[r, side, :c]
-        return v
+        return [v[t] + corrections[t] for t in range(8)]
 
     def advect(v):
         dx = along_x(v, fwd_ref)
@@ -566,14 +589,26 @@
     total_div = assemble(div, 4, put_advected)
     r0 = [total_div[t] * (quad[t] * (-1.0 / time_step)) for t in range(8)]
 
-    def local(v):
-        dx = along_x(v, fwd_ref)
-        dy = along_y(v, deriv, -1)
-        dz = along_index(deriv, -1, v)
-        bx = along_x([mobile[t] * dx[t] for t in range(8)], bwd_ref)
-        by = along_y([mobile[t] * dy[t] for t in range(8)], deriv_t, -1)
-        bz = along_index(deriv_t, -1, [mobile[t] * dz[t] for t in range(8)])
+    def slopes(v):
+        return along_x(v, fwd_ref), along_y(v, deriv, -1), along_index(deriv, -1, v)
+
+    def flux(slope):
+        return [[mobile[t] * part[t] for t in range(8)] for part in slope]
+
+    def local(v, flow):
+        bx = along_x(flow[0], bwd_ref)
+        by = along_y(flow[1], deriv_t, -1)
+        bz = along_index(deriv_t, -1, flow[2])
         return [(mass_shift * quad[t]) * v[t] + bx[t] + by[t] + bz[t] for t in range(8)]
+
+    def energy_row(v, slope, flow):
+        acc = None
+        for t in range(8):
+            term = (mass_shift * quad[t]) * (v[t] * v[t])
+            for i in range(3):
+                term = term + flow[i][t] * slope[i][t]
+            acc = term if acc is None else acc + term
+        return jnp.sum(acc[0], axis=0, keepdims=True)
 
     def dot_row(a, b, scale=None):
         acc = None
@@ -593,14 +628,17 @@
         given["s"], given["w"] = give(s, w)
 
     z0 = [r0[t] * inverse_jacobi[t] for t in range(8)]
-    lz = local(z0)
+    slope = slopes(z0)
+    flow = flux(slope)
+    lz = local(z0, flow)
     rho_row = dot_row(r0, z0, share)
-    gamma_row = dot_row(z0, lz)
+    gamma_row = energy_row(z0, slope, flow)
     s = assemble(lz, 5, give_first)
     w = [s[t] * inverse_jacobi[t] for t in range(8)]
-    lw = local(w)
     delta_row = dot_row(s, w, share)
-    eps_row = dot_row(w, lw)
+    slope = slopes(w)
+    flow = flux(slope)
+    eps_row = energy_row(w, slope, flow)
     partial = jnp.concatenate(
         [rho_row, gamma_row, delta_row, eps_row, jnp.zeros((4, 128), f32)], axis=0
     )
@@ -619,7 +657,7 @@
         ).start()
 
     each_other(share_sums)
-    t_vec = assemble(lw, 6, give_second)
+    t_vec = assemble(local(w, flow), 6, give_second)
     third, _ = give(t_vec, t_vec)
     arrived = pltpu.make_async_remote_copy(
         src_ref=sums_in,
@@ -629,6 +667,8 @@
         device_id=tuple(lax.rem(me[i] + 1, counts[i]) for i in range(3)),
         device_id_type=MESH,
     )
+    sent()
+    arrived.wait_send()
     arrived.wait_recv()
     joined = own + jnp.sum(sums_in[...], axis=0)
     four = jnp.sum(jnp.where(sub8 == lane8, joined, 0.0), axis=1, keepdims=True)
@@ -645,8 +685,6 @@
 
     pre_ref[...] = along * given["z0"] - side_step * given["w"]
     res_ref[...] = given["r0"] - along * given["s"] + side_step * third
-    sent()
-    arrived.wait_send()
 
 
 def finish_kernel(adv_ref, pre_ref, res_ref, adv_out, pre_out, res_out):
@@ -680,7 +718,7 @@
             faces,
             faces,
             faces_z,
-            pltpu.VMEM((ROUNDS, 8, 1, 128), f32),
+            pltpu.VMEM((ROUNDS, 12, 1, 128), f32),
             pltpu.VMEM((ROUNDS, 9, 8, 128), f32),
             faces_z,
             pltpu.VMEM((ROUNDS, 27, 1, 128), f32),

time: 36.3 us -> 34.9 us (0.961)
  Pallas kernels: 35.5 us -> 34.1 us
    pallas_call x1, Pallas kernels: 34.8 us -> 33.5 us  [per_device(): pl.pallas_call(functools.partial(kernel, counts), out_shape=shapes, in_sp...]
where the time goes in v4:
time: 34.9 us; the launch traced here: 34.8 us
  Pallas kernels  34.1 us (98%)
  between operations  0.64 us (2%)
    pallas_call x1, Pallas kernels, per_device(): pl.pallas_call(functools.partial(kernel, counts), out_shape=shapes, in_sp...  33.5 us

profile of v4, /device:TPU:0, one launch (start us, length us, event | category | flops | bytes accessed | tf_op | source)
XLA Modules:
  0.0 34.8 jit_solution(4020868483298611211)
XLA Ops:
  0.6 33.5 %shard_map.94 = (f32[3,16,512]{2,1,0:T(8,128)S(1)}, f32[16,512]{1,0:T(8,128)S(1)}, f32[16,512]{1,0:T(8,128)S(1)}) custom-call(f32[3,16,512]{2,1,0:T(8,128)} %bitcast.5, f32[16,512]{1,0:T(8,128)} %bitcast.6, s32[16]{0:T(128)} %place_hbm.1, f32[8,128]{1,0:T(8,128)} %constant.8.clone.plane_hbm, bf16[384,128]{1,0:T(8,128)(2,1)} %constant.9.clone.fwd_hbm, ...), custom_call_target="tpu_custom_call" | custom-call | tf_op jit(solution)/shard_map/pallas_call | solution.py:712
  34.1 0.7 %shard_map.95 = (f32[3,16,512]{2,1,0:T(8,128)}, f32[16,512]{1,0:T(8,128)}, f32[16,512]{1,0:T(8,128)}) custom-call(f32[3,16,512]{2,1,0:T(8,128)S(1)} %get-tuple-element.9.adv_ref, f32[16,512]{1,0:T(8,128)S(1)} %get-tuple-element.10.pre_ref, f32[16,512]{1,0:T(8,128)S(1)} %get-tuple-element.11.res_ref), custom_call_target="tpu_custom_call" | custom-call | tf_op jit(solution)/shard_map/pallas_call | solution.py:761

commit v5 on v4

--- a/solution.py
+++ b/solution.py
@@ -189,9 +189,10 @@
     peers = {d: (exists(d), tuple(me[i] + d[i] for i in range(3))) for d in directions}
     far = [d for d in directions if d[1] and d[2]]
     far.sort(key=lambda d: abs(d[0]))
-    near_edges = [d for d in directions if d[0] and d[2] and not d[1]]
-    near = [d for d in directions if d not in far and d not in near_edges]
-    near.sort(key=lambda d: (-abs(d[2]), -abs(d[1]), abs(d[0])))
+    up_down = [(0, 0, -1), (0, 0, 1)]
+    cross = [d for d in directions if d[0] and d[2] and not d[1]]
+    flat = [d for d in directions if not d[2]]
+    flat.sort(key=lambda d: (-abs(d[1]), abs(d[0])))
 
     barrier = pltpu.get_barrier_semaphore()
 
@@ -222,6 +223,13 @@
     join_low_y, join_high_y = (sub8 == 0) & (ey > 0), (sub8 == 7) & (ey < 3)
     pack_b = lane8 // 16
     pack_low_y, pack_high_y = (pack_b == 0) & (ey > 0), (pack_b == 7) & (ey < 3)
+    origin = [(lane8 - 3 - (lane8 + 1) % 4) % 128, (lane8 + 3 - lane8 % 4) % 128]
+    edge_join_low = [(o < 16) & ((o // 4) % 4 > 0) for o in origin]
+    edge_join_high = [(o >= 112) & ((o // 4) % 4 < 3) for o in origin]
+    far_y = ((sub8 == 0) & (ey == 0)) | ((sub8 == 7) & (ey == 3))
+    far_low = (sub8 == 0) & ((lane8 == 0) | (lane8 == 124))
+    far_high = (sub8 == 7) & ((lane8 == 3) | (lane8 == 127))
+    far_corner = far_low | far_high
     edge_low_y, edge_high_y = (pack_b == 0) & (ey == 0), (pack_b == 7) & (ey == 3)
 
     def half(flag):
@@ -272,12 +280,18 @@
     for e in range(16):
         by_lane = jnp.where(l16 == e, place_ref[e], by_lane)
         by_row = jnp.where(r16 == e, place_ref[e], by_row)
-    to_place = (by_lane == r16).astype(f32)
-    to_slot = (by_row == l16).astype(f32)
+    to_place = jnp.concatenate([(by_lane == r16).astype(f32)] * 3, axis=1)
+    to_slot = jnp.concatenate([(by_row == l16).astype(f32)] * 3, axis=1)
 
     def order(matrix, block):
+        high = block.astype(jnp.bfloat16).astype(f32)
+        rest = block - high
+        middle = rest.astype(jnp.bfloat16).astype(f32)
+        parts = jnp.concatenate([high, middle, rest - middle], axis=0)
         return jnp.dot(
-            matrix, block, precision=lax.Precision.HIGHEST, preferred_element_type=f32
+            matrix.astype(jnp.bfloat16),
+            parts.astype(jnp.bfloat16),
+            preferred_element_type=f32,
         )
 
     lane64 = lax.broadcasted_iota(jnp.int32, (64, 128), 1)
@@ -331,12 +345,6 @@
         low = (x - high.astype(f32)).astype(jnp.bfloat16)
         return jnp.concatenate([high, low, high], axis=1)
 
-    def along_x(v, w_ref):
-        c = v[0].shape[0]
-        x = jnp.concatenate([v[t].reshape(c * 8, 128) for t in range(8)], axis=0)
-        y = jnp.dot(split(x), w_ref[...], preferred_element_type=f32)
-        return [y[t * c * 8 : (t + 1) * c * 8].reshape(c, 8, 128) for t in range(8)]
-
     def along_y(v, matrix, sign):
         c = v[0].shape[0]
         put_planes(work_v, v)
@@ -352,12 +360,16 @@
     def column(dx, dy):
         return 3 * (dx + 1) + dy + 1
 
+    def edge_slot(d):
+        if d[0] and d[1]:
+            return 8 + 4 * side_of(d[0]) + 2 * side_of(d[1]) + side_of(d[2])
+        return (0 if d[0] else 4) + 2 * side_of(d[0] or d[1]) + side_of(d[2])
+
     def source(r, d, c):
         if not d[0] and not d[1]:
             return send_z.at[r, side_of(d[2]), pl.ds(0, c)]
         if d[2]:
-            kind = (8 if d[1] else 0) if d[0] else 4
-            return send_e.at[r, kind + 2 * side_of(d[0] or d[1]) + side_of(d[2])]
+            return send_e.at[r, edge_slot(d)]
         return (send_x if d[0] else send_y).at[r, side_of(d[0] if d[0] else d[1])]
 
     def target(r, d, c):
@@ -433,6 +445,17 @@
         low, high = turn(turn(v, 1, 1), 1, 2), turn(turn(v, -1, 1), -1, 2)
         return v + jnp.where(join_low_y, low, jnp.where(join_high_y, high, 0.0))
 
+    def join_xy(v):
+        up, down = turn(v, 1, 1), turn(v, -1, 1)
+        low, high = turn(v, 20, 2), turn(v, -20, 2)
+        out = v + jnp.where(join_low_x, low, jnp.where(join_high_x, high, 0.0))
+        for face, step, mask in ((up, 1, join_low_y), (down, -1, join_high_y)):
+            part = turn(face, step, 2)
+            low, high = turn(face, step + 20, 2), turn(face, step - 20, 2)
+            part = part + jnp.where(join_low_x, low, jnp.where(join_high_x, high, 0.0))
+            out = out + jnp.where(mask, part, 0.0)
+        return out
+
     def merge(parts, index, bit=1):
         while len(parts) > 1:
             parts = [
@@ -452,8 +475,54 @@
         low, high = recv_e[r, code((dx, dy, -1))], recv_e[r, code((dx, dy, 1))]
         return jnp.where(sub8 == 0, low, jnp.where(sub8 == 7, high, 0.0))
 
+    def send_far(r, dz, v):
+        c = v.shape[0]
+        for side, dy in enumerate((-1, 1)):
+            shift = -3 * dy if side else 3
+            slot = (ey + 1 - side) % 4
+            face = by_slot([turn(v[k], k + shift, 1) for k in range(c)], slot)
+            low = by_slot([turn(v[k], k + shift + 20, 1) for k in range(c)], slot)
+            high = by_slot([turn(v[k], k + shift - 20, 1) for k in range(c)], slot)
+            face = face + jnp.where(
+                edge_join_low[side], low, jnp.where(edge_join_high[side], high, 0.0)
+            )
+            row = 7 * side
+            send_e[r, edge_slot((0, dy, dz))] = face[row : row + 1]
+            for dx in (-1, 1):
+                shift_x = -124 * dx - 3 * dy
+                corner = by_slot(
+                    [turn(v[k], shift_x + 16 * k, 1) for k in range(c)],
+                    ((lane8 + 4) // 16) % 8,
+                )
+                send_e[r, edge_slot((dx, dy, dz))] = corner[row : row + 1]
+
+    def take_far(r, dz, c):
+        face = jnp.where(
+            sub8 == 0,
+            recv_e[r, code((0, -1, dz))],
+            jnp.where(sub8 == 7, recv_e[r, code((0, 1, dz))], 0.0),
+        )
+        inner = lane8 % 16 < 4
+        rows = [
+            jnp.where(inner, recv_e[r, code((-1, dy, dz))], recv_e[r, code((1, dy, dz))])
+            for dy in (-1, 1)
+        ]
+        corner = jnp.where(sub8 == 0, rows[0], jnp.where(sub8 == 7, rows[1], 0.0))
+        return jnp.stack(
+            [
+                jnp.where(far_y, turn(face, -k, 1), 0.0)
+                + jnp.where(far_corner, turn(corner, -16 * k, 1), 0.0)
+                for k in range(c)
+            ]
+        )
+
     def assemble(v, r, hook=None):
+        for side in range(2):
+            send_far(r, 2 * side - 1, v[7 * side])
         c = v[0].shape[0]
+        for side in range(2):
+            send_z[r, side, pl.ds(0, c)] = v[7 * side]
+        v = list(v)
         put_planes(work_g, v)
         rows = [
             [work_g[k, pl.ds(b, 8, stride=8), :] for k in range(c)] for b in range(8)
@@ -463,72 +532,62 @@
             face = by_slot([turn(own[k], k - 3 * side, 1) for k in range(c)], ey)
             low = by_slot([turn(own[k], k - 3 * side + 20, 1) for k in range(c)], ey)
             high = by_slot([turn(own[k], k - 3 * side - 20, 1) for k in range(c)], ey)
-            face = face + jnp.where(join_low_x, low, jnp.where(join_high_x, high, 0.0))
-            send_y[r, side] = face
-            send_e[r, 4 + 2 * side] = face[0:1]
-            send_e[r, 5 + 2 * side] = face[7:8]
-
-        def pack(side, b):
-            shift = 16 * b - 124 * side
-            return by_slot([turn(rows[b][k], shift + 4 * k, 1) for k in range(c)], ex)
-
-        packed = [[pack(side, b) if b in (0, 7) else None for b in range(8)] for side in range(2)]
+            send_y[r, side] = face + jnp.where(
+                join_low_x, low, jnp.where(join_high_x, high, 0.0)
+            )
+        start(r, c, far + flat[:2] + up_down)
         for side in range(2):
-            corner = jnp.where(pack_b < 4, packed[side][0], packed[side][7])
-            send_e[r, 8 + 2 * side] = corner[0:1]
-            send_e[r, 9 + 2 * side] = corner[7:8]
-        start(r, c, far)
-        v = list(v)
-        for side in range(2):
-            v[7 * side] = join_x(join_y(v[7 * side]))
-            send_z[r, side, pl.ds(0, c)] = v[7 * side]
-        for side in range(2):
-            face = merge(
-                [packed[side][b] if b in (0, 7) else pack(side, b) for b in range(8)], pack_b
-            )
-            low, high = turn(face, 17, 1), turn(face, -17, 1)
+            packed = []
+            for b in range(8):
+                shift = 16 * b - 124 * side
+                packed.append(by_slot([turn(rows[b][k], shift + 4 * k, 1) for k in range(c)], ex))
+            face = merge(packed, pack_b)
+            shift = -124 * side
+            low = by_slot([turn(rows[7][k], shift + 4 * k + 1, 1) for k in range(c)], ex)
+            shift += 112
+            high = by_slot([turn(rows[0][k], shift + 4 * k - 1, 1) for k in range(c)], ex)
             face = face + jnp.where(pack_low_y, low, jnp.where(pack_high_y, high, 0.0))
             send_x[r, side] = face
             send_e[r, 2 * side] = face[0:1]
             send_e[r, 2 * side + 1] = face[7:8]
-        start(r, c, near_edges + near)
+        start(r, c, cross + flat[2:])
         for t in range(1, 7):
             v[t] = join_x(join_y(v[t]))
         if hook is not None:
             hook()
-        finish(r, c, near)
-        faces = []
-        for dx in (-1, 1):
-            low = turn(recv_xy[r, column(dx, -1)], 13, 1)
-            high = turn(recv_xy[r, column(dx, 1)], -13, 1)
-            faces.append(
-                recv_xy[r, column(dx, 0)]
-                + jnp.where(edge_low_y, low, jnp.where(edge_high_y, high, 0.0))
-            )
+        finish(r, c, flat + up_down + cross)
+        faces = [recv_xy[r, column(dx, 0)] + edge_rows(r, dx, 0) for dx in (-1, 1)]
         for side in range(2):
-            v[7 * side] = v[7 * side] + recv_z[r, side, :c]
-        finish(r, c, far + near_edges)
-        faces = [faces[i] + edge_rows(r, 2 * i - 1, 0) for i in range(2)]
-        sides = [recv_xy[r, column(0, dy)] + edge_rows(r, 0, dy) for dy in (-1, 1)]
-        corners = [[edge_rows(r, dx, dy) for dx in (-1, 1)] for dy in (-1, 1)]
-        for b in (0, 7, 1, 2, 3, 4, 5, 6):
+            v[7 * side] = join_xy(v[7 * side] + recv_z[r, side, :c])
+        for b in range(8):
             for k in range(c):
                 low = turn(faces[0], -16 * b - 4 * k, 1)
                 high = turn(faces[1], 124 - 16 * b - 4 * k, 1)
                 part = jnp.where(lane8 < 4, low, jnp.where(lane8 >= 124, high, 0.0))
                 if b in (0, 7):
                     side = b // 7
-                    slot = 3 * side
-                    part = part + jnp.where(ey == slot, turn(sides[side], slot - k, 1), 0.0)
+                    dy, slot = 2 * side - 1, 3 * side
+                    face = turn(recv_xy[r, column(0, dy)], slot - k, 1)
+                    part = part + jnp.where(ey == slot, face, 0.0)
                     begin = slot - 4 * k - 115 * (1 - side)
-                    low = turn(corners[side][0], begin, 1)
-                    high = turn(corners[side][1], begin + 124, 1)
+                    low = turn(recv_xy[r, column(-1, dy)], begin, 1)
+                    high = turn(recv_xy[r, column(1, dy)], begin + 124, 1)
                     part = part + jnp.where(
                         lane8 == slot, low, jnp.where(lane8 == 124 + slot, high, 0.0)
                     )
                 work_c[k, pl.ds(b, 8, stride=8), :] = part
         corrections = planes_of(work_c, c)
-        return [v[t] + corrections[t] for t in range(8)]
+        v = [v[t] + corrections[t] for t in range(8)]
+        finish(r, c, far)
+        for side in range(2):
+            v[7 * side] = v[7 * side] + take_far(r, 2 * side - 1, c)
+        return v
+
+    def along_x(v, w_ref):
+        c = v[0].shape[0]
+        x = jnp.concatenate([v[t].reshape(c * 8, 128) for t in range(8)], axis=0)
+        y = jnp.dot(split(x), w_ref[...], preferred_element_type=f32)
+        return [y[t * c * 8 : (t + 1) * c * 8].reshape(c, 8, 128) for t in range(8)]
 
     def advect(v):
         dx = along_x(v, fwd_ref)
@@ -540,7 +599,6 @@
         ]
 
     loads[3].wait()
-    first = advect(velocity)
     diag, quad, mobile = [], [], []
 
     def diagonal():
@@ -557,25 +615,20 @@
             mass_shift * quad[t] + square_x[t] + square_y[t] + square_z[t] for t in range(8)
         )
 
+    rate = advect(velocity)
     pl.semaphore_wait(barrier, others)
-    first = assemble(first, 0, diagonal)
-    k1 = [first[t] * share[t] for t in range(8)]
-    total_rate = k1
-    v = [velocity[t] - (0.5 * time_step) * k1[t] for t in range(8)]
-    for r, step, weight in ((1, 0.5, 2.0), (2, 1.0, 2.0), (3, 0.0, 1.0)):
-        g = advect(v)
+    total_rate = None
+    for r, step, weight in ((0, 0.5, 1.0), (1, 0.5, 2.0), (2, 1.0, 2.0), (3, 0.0, 1.0)):
         if r == 1:
-            g = assemble([jnp.concatenate([g[t], diag[t]], axis=0) for t in range(8)], r)
+            rate = [jnp.concatenate([rate[t], diag[t]], axis=0) for t in range(8)]
+        g = assemble(rate, r, None if r else diagonal)
+        if r == 1:
             inverse_jacobi = [1.0 / g[t][3:4] for t in range(8)]
-            g = [g[t][0:3] for t in range(8)]
-        else:
-            g = assemble(g, r)
-        g = [g[t] * share[t] for t in range(8)]
-        total_rate = [total_rate[t] + weight * g[t] for t in range(8)]
+        g = [g[t][0:3] * share[t] for t in range(8)]
+        total_rate = [weight * g[t] + (total_rate[t] if r else 0.0) for t in range(8)]
         if step:
-            v = [velocity[t] - (step * time_step) * g[t] for t in range(8)]
+            rate = advect([velocity[t] - (step * time_step) * g[t] for t in range(8)])
     advected = [velocity[t] - (time_step / 6.0) * total_rate[t] for t in range(8)]
-
     div_x = along_x([advected[t][0:1] for t in range(8)], fwd_ref)
     div_y = along_y([advected[t][1:2] for t in range(8)], deriv, -1)
     div_z = along_index(deriv, -1, [advected[t][2:3] for t in range(8)])
@@ -630,10 +683,10 @@
     z0 = [r0[t] * inverse_jacobi[t] for t in range(8)]
     slope = slopes(z0)
     flow = flux(slope)
-    lz = local(z0, flow)
     rho_row = dot_row(r0, z0, share)
     gamma_row = energy_row(z0, slope, flow)
-    s = assemble(lz, 5, give_first)
+
+    s = assemble(local(z0, flow), 5, give_first)
     w = [s[t] * inverse_jacobi[t] for t in range(8)]
     delta_row = dot_row(s, w, share)
     slope = slopes(w)
@@ -718,7 +771,7 @@
             faces,
             faces,
             faces_z,
-            pltpu.VMEM((ROUNDS, 12, 1, 128), f32),
+            pltpu.VMEM((ROUNDS, 16, 1, 128), f32),
             pltpu.VMEM((ROUNDS, 9, 8, 128), f32),
             faces_z,
             pltpu.VMEM((ROUNDS, 27, 1, 128), f32),

time: 34.9 us -> 34.8 us (level)
  no operation moved by 1% of the time
where the time goes in v5:
time: 34.8 us; the launch traced here: 34.6 us
  Pallas kernels  34 us (98%)
  between operations  0.64 us (2%)
    pallas_call x1, Pallas kernels, per_device(): pl.pallas_call(functools.partial(kernel, counts), out_shape=shapes, in_sp...  33.3 us

profile of v5, /device:TPU:0, one launch (start us, length us, event | category | flops | bytes accessed | tf_op | source)
XLA Modules:
  0.0 34.6 jit_solution(2706379673123805199)
XLA Ops:
  0.6 33.3 %shard_map.94 = (f32[3,16,512]{2,1,0:T(8,128)S(1)}, f32[16,512]{1,0:T(8,128)S(1)}, f32[16,512]{1,0:T(8,128)S(1)}) custom-call(f32[3,16,512]{2,1,0:T(8,128)} %bitcast.5, f32[16,512]{1,0:T(8,128)} %bitcast.6, s32[16]{0:T(128)} %place_hbm.1, f32[8,128]{1,0:T(8,128)} %constant.8.clone.plane_hbm, bf16[384,128]{1,0:T(8,128)(2,1)} %constant.9.clone.fwd_hbm, ...), custom_call_target="tpu_custom_call" | custom-call | tf_op jit(solution)/shard_map/pallas_call | solution.py:765
  34.0 0.7 %shard_map.95 = (f32[3,16,512]{2,1,0:T(8,128)}, f32[16,512]{1,0:T(8,128)}, f32[16,512]{1,0:T(8,128)}) custom-call(f32[3,16,512]{2,1,0:T(8,128)S(1)} %get-tuple-element.9.adv_ref, f32[16,512]{1,0:T(8,128)S(1)} %get-tuple-element.10.pre_ref, f32[16,512]{1,0:T(8,128)S(1)} %get-tuple-element.11.res_ref), custom_call_target="tpu_custom_call" | custom-call | tf_op jit(solution)/shard_map/pallas_call | solution.py:814

commit v6 on v5

--- a/solution.py
+++ b/solution.py
@@ -145,7 +145,7 @@
             )
         )
     ]
-    for load in loads:
+    for load in loads[:2]:
         load.start()
     me = [lax.axis_index(name) for name in AXES]
     has = [(me[i] > 0, me[i] < counts[i] - 1) for i in range(3)]
@@ -200,7 +200,7 @@
         pl.semaphore_signal(barrier, inc=1, device_id=device, device_id_type=MESH)
 
     if max(counts) <= ROUNDS:
-        for d in directions:
+        for d in far[::-1] + cross + up_down + flat:
 
             @pl.when(peers[d][0])
             def _():
@@ -214,6 +214,9 @@
     else:
         each_other(greet)
         others = counts[0] * counts[1] * counts[2] - 1
+
+    for load in loads[2:]:
+        load.start()
 
     sub8 = lax.broadcasted_iota(jnp.int32, (8, 128), 0)
     lane8 = lax.broadcasted_iota(jnp.int32, (8, 128), 1)

time: 34.8 us -> 34.8 us (level)
  no operation moved by 1% of the time
where the time goes in v6:
time: 34.8 us; the launch traced here: 34.7 us
  Pallas kernels  34 us (98%)
  between operations  0.64 us (2%)
    pallas_call x1, Pallas kernels, per_device(): pl.pallas_call(functools.partial(kernel, counts), out_shape=shapes, in_sp...  33.4 us

profile of v6, /device:TPU:0, one launch (start us, length us, event | category | flops | bytes accessed | tf_op | source)
XLA Modules:
  0.0 34.7 jit_solution(1820150785269562798)
XLA Ops:
  0.6 33.4 %shard_map.94 = (f32[3,16,512]{2,1,0:T(8,128)S(1)}, f32[16,512]{1,0:T(8,128)S(1)}, f32[16,512]{1,0:T(8,128)S(1)}) custom-call(f32[3,16,512]{2,1,0:T(8,128)} %bitcast.5, f32[16,512]{1,0:T(8,128)} %bitcast.6, s32[16]{0:T(128)} %place_hbm.1, f32[8,128]{1,0:T(8,128)} %constant.8.clone.plane_hbm, bf16[384,128]{1,0:T(8,128)(2,1)} %constant.9.clone.fwd_hbm, ...), custom_call_target="tpu_custom_call" | custom-call | tf_op jit(solution)/shard_map/pallas_call | solution.py:768
  34.0 0.7 %shard_map.95 = (f32[3,16,512]{2,1,0:T(8,128)}, f32[16,512]{1,0:T(8,128)}, f32[16,512]{1,0:T(8,128)}) custom-call(f32[3,16,512]{2,1,0:T(8,128)S(1)} %get-tuple-element.9.adv_ref, f32[16,512]{1,0:T(8,128)S(1)} %get-tuple-element.10.pre_ref, f32[16,512]{1,0:T(8,128)S(1)} %get-tuple-element.11.res_ref), custom_call_target="tpu_custom_call" | custom-call | tf_op jit(solution)/shard_map/pallas_call | solution.py:817
